TPU v7x, 256 devices: a whole 4x4x8 slice. The times are simulated.
256 devices in a mesh: dp: 4 (over y_lo, core), sp: 8 (over y_hi, x), tp: 8 (over z).
Axes of the slice: x: 4, y: 4 (y_hi: 2, y_lo: 2; y = y_hi * 2 + y_lo), z: 8, core: 2. Of those that a mesh axis runs over, the one named last changes fastest.
Arguments:
- query: bfloat16 [4, 3072, 3072], P('dp', 'sp', 'tp'), may hold values from -110 to 110
- key: bfloat16 [4, 3072, 3072], P('dp', 'sp', 'tp'), may hold values from -8 to 8
- value: bfloat16 [4, 3072, 3072], P('dp', 'sp', 'tp'), may hold values from -6 to 6
- text_key: bfloat16 [4, 256, 3072], P('dp', None, 'tp'), may hold values from -6 to 6
- text_value: bfloat16 [4, 256, 3072], P('dp', None, 'tp'), may hold values from -6 to 6
- grad_out: bfloat16 [4, 3072, 3072], P('dp', 'sp', 'tp'), may hold values from -6 to 6
- gate: bfloat16 [4, 3072], P('dp'), may hold values from 0.5 to 1.5
- out_weight: bfloat16 [3072, 3072], P('tp', 'dp'), may hold values from -0.109375 to 0.109375
- windows: int32 [8, 2], P('sp'), may hold values from 0 to 2, as said below
- tile_map: int32 [8, 1], replicated, may hold values from 0 to 2, as said below
- text_count: int32 [4], P('dp'), may hold values from 1 to 256
Outputs:
- grad_query: bfloat16 [4, 3072, 3072], P('dp', 'sp', 'tp')
- grad_key: bfloat16 [4, 3072, 3072], P('dp', 'sp', 'tp')
- grad_value: bfloat16 [4, 3072, 3072], P('dp', 'sp', 'tp')
- grad_text_key: bfloat16 [4, 256, 3072], P('dp', None, 'tp')
- grad_text_value: bfloat16 [4, 256, 3072], P('dp', None, 'tp')
- grad_weight: float32 [3072, 3072], P('tp', 'dp')
Inputs may be any that keep to these rules, and one draw needn't show every extreme that they name: `tile_map`: the positions within each row are distinct. `windows`: the time reach is 0 or 1; the first tile of every time slab has time reach 1 and spatial reach 2.
All inputs are finite; a program needn't handle non-finite values.
Results may differ from a plain program's by a relative error of at most 0.024.
Values may be sent and summed in bfloat16 or wider, within the bound.
A program may use at most 64 MiB of HBM per device.

v0:
```python
import jax
import jax.numpy as jnp
from jax import lax
from jax.sharding import PartitionSpec as P

HD = 128
TILE = 384


def in_order(parts, dim):
    shape = list(parts.shape[1:])
    shape[dim] *= parts.shape[0]
    return jnp.moveaxis(parts, 0, dim).reshape(shape)


def from_everyone(shard, axis):
    copies = jnp.broadcast_to(shard, (lax.axis_size(axis), *shard.shape))
    return lax.all_to_all(copies, axis, split_axis=0, concat_axis=0, tiled=True)


def gathered_copies(shard, axis, dim):
    return in_order(from_everyone(shard, axis), dim)


def padded(cells, sides, width):
    for axis, dim in sides:
        count = lax.axis_size(axis)
        ends = count - 1
        head = lax.slice_in_dim(cells, 0, width, axis=dim)
        tail = lax.slice_in_dim(cells, cells.shape[dim] - width, cells.shape[dim], axis=dim)
        cells = jnp.concatenate(
            [
                lax.ppermute(tail, axis, [(i, (i + 1) % count) for i in range(ends)]),
                cells,
                lax.ppermute(head, axis, [((i + 1) % count, i) for i in range(ends)]),
            ],
            axis=dim,
        )
    return cells


def shifted(block, axis, distance):
    devices = range(lax.axis_size(axis))
    route = [(i - distance, i) for i in devices if i - distance in devices]
    return lax.ppermute(block, axis, route)


def cut_along(shard, dim, count):
    shape = shard.shape
    parts = shard.reshape(*shape[:dim], count, shape[dim] // count, *shape[dim + 1 :])
    return jnp.moveaxis(parts, dim, 0)


def summed_on_arrival(shard, axis, dim):
    count = lax.axis_size(axis)
    parts = lax.all_to_all(cut_along(shard, dim, count), axis, 0, 0, tiled=True)
    return jnp.sum(parts.astype(jnp.float32), axis=0)


def window_mask(own_map, side_maps, valid, spans, text_live):
    reach = jnp.abs(jnp.arange(3, dtype=jnp.int32) - 1)
    near_time = reach[None, :, None] <= spans[:, 0][:, None, None]
    near_space = (
        jnp.abs(own_map[:, None, None] - side_maps[None, :, :]) <= spans[:, 1][:, None, None]
    )
    allowed = near_time & near_space & valid[None, :, None]
    count = own_map.shape[0]
    tiles = allowed.reshape(count, 3 * count)
    video = jnp.broadcast_to(tiles[:, None, :, None], (count, TILE, 3 * count, TILE))
    video = video.reshape(count * TILE, 3 * count * TILE)
    text = jnp.broadcast_to(text_live[None, :], (count * TILE, text_live.shape[0]))
    return jnp.concatenate([video, text], axis=1)


def tile_attention(query, keys, values, grad_attn, allowed):
    factor = HD ** (-0.5)
    scores = factor * jnp.dot(query, keys.T, preferred_element_type=jnp.float32)
    scores = jnp.where(allowed, scores, -1e30)
    top = jnp.max(scores, axis=1, keepdims=True)
    weights = jnp.exp(scores - top)
    weights = weights / jnp.sum(weights, axis=1, keepdims=True)
    probs = weights.astype(jnp.bfloat16)
    attended = jnp.dot(probs, values, preferred_element_type=jnp.float32).astype(jnp.bfloat16)
    delta = jnp.sum(
        grad_attn.astype(jnp.float32) * attended.astype(jnp.float32), axis=1, keepdims=True
    )
    grad_probs = jnp.dot(grad_attn, values.T, preferred_element_type=jnp.float32)
    grad_scores = (weights * (grad_probs - delta)).astype(jnp.bfloat16)
    grad_query = factor * jnp.dot(grad_scores, keys, preferred_element_type=jnp.float32)
    grad_keys = factor * jnp.dot(grad_scores.T, query, preferred_element_type=jnp.float32)
    grad_values = jnp.dot(probs.T, grad_attn, preferred_element_type=jnp.float32)
    return (attended, grad_query, grad_keys, grad_values)


def per_device(
    query,
    key,
    value,
    text_key,
    text_value,
    grad_out,
    gate,
    out_weight,
    windows,
    tile_map,
    text_count,
):
    own_query = query[0]
    tok = own_query.shape[0]
    width = own_query.shape[1]
    full_grad = lax.all_gather(grad_out[0], "tp", axis=1, tiled=True)
    scaled = (full_grad.astype(jnp.float32) * gate[0].astype(jnp.float32)[None, :]).astype(
        jnp.bfloat16
    )
    grad_attn = lax.dot_general(
        scaled,
        gathered_copies(out_weight, "dp", 1),
        (((1,), (1,)), ((), ())),
        preferred_element_type=jnp.float32,
    )
    grad_attn = grad_attn.astype(jnp.bfloat16)
    paired = jnp.stack([key[0], value[0]], axis=0)
    extended = padded(paired, (("sp", 1),), tok)
    index = lax.axis_index("sp")
    slabs = lax.axis_size("sp")
    tiles_here = tile_map.shape[1]
    blank = jnp.zeros((1, tiles_here), jnp.int32)
    padded_map = jnp.concatenate([blank, tile_map, blank], axis=0)
    own_map = lax.dynamic_index_in_dim(tile_map, index, 0, keepdims=False)
    side_maps = lax.dynamic_slice_in_dim(padded_map, index, 3, 0)
    others = index + jnp.arange(3, dtype=jnp.int32) - 1
    valid = (others >= 0) & (others < slabs)
    text_live = jnp.arange(text_key.shape[1], dtype=jnp.int32) < text_count[0]
    allowed = window_mask(own_map, side_maps, valid, windows, text_live)
    results = [[], [], [], []]
    for head in range(width // HD):
        lower = head * HD
        upper = lower + HD
        all_k = jnp.concatenate([extended[0][:, lower:upper], text_key[0][:, lower:upper]], axis=0)
        all_v = jnp.concatenate(
            [extended[1][:, lower:upper], text_value[0][:, lower:upper]], axis=0
        )
        outcome = tile_attention(
            own_query[:, lower:upper], all_k, all_v, grad_attn[:, lower:upper], allowed
        )
        for place in range(4):
            results[place].append(outcome[place])
    attended = jnp.concatenate(results[0], axis=1)
    grad_q = jnp.concatenate(results[1], axis=1)
    grad_k = jnp.concatenate(results[2], axis=1)
    grad_v = jnp.concatenate(results[3], axis=1)
    earlier = jnp.stack([grad_k[:tok], grad_v[:tok]], axis=0)
    later = jnp.stack([grad_k[2 * tok : 3 * tok], grad_v[2 * tok : 3 * tok]], axis=0)
    from_later = shifted(earlier.astype(jnp.bfloat16), "sp", -1).astype(earlier.dtype)
    from_earlier = shifted(later.astype(jnp.bfloat16), "sp", 1).astype(later.dtype)
    own_k = grad_k[tok : 2 * tok] + from_later[0] + from_earlier[0]
    own_v = grad_v[tok : 2 * tok] + from_later[1] + from_earlier[1]
    text_k, text_v = (
        lax.psum(grad_k[3 * tok :].astype(jnp.bfloat16), "sp").astype(jnp.float32),
        lax.psum(grad_v[3 * tok :].astype(jnp.bfloat16), "sp").astype(jnp.float32),
    )
    local_weight = lax.dot_general(
        attended, scaled, (((0,), (0,)), ((), ())), preferred_element_type=jnp.float32
    )
    spread = summed_on_arrival(local_weight.astype(jnp.bfloat16), ("dp", "sp"), 1)
    weight_grad = gathered_copies(spread, "sp", 1)
    return (
        grad_q.astype(jnp.bfloat16)[None],
        own_k.astype(jnp.bfloat16)[None],
        own_v.astype(jnp.bfloat16)[None],
        text_k.astype(jnp.bfloat16)[None],
        text_v.astype(jnp.bfloat16)[None],
        weight_grad,
    )


def solution(mesh):
    placed = (
        P("dp", "sp", "tp"),
        P("dp", "sp", "tp"),
        P("dp", "sp", "tp"),
        P("dp", None, "tp"),
        P("dp", None, "tp"),
        P("dp", "sp", "tp"),
        P("dp", None),
        P("tp", "dp"),
        P("sp", None),
        P(),
        P("dp"),
    )
    return jax.shard_map(
        per_device,
        mesh=mesh,
        in_specs=placed,
        out_specs=(
            P("dp", "sp", "tp"),
            P("dp", "sp", "tp"),
            P("dp", "sp", "tp"),
            P("dp", None, "tp"),
            P("dp", None, "tp"),
            P("tp", "dp"),
        ),
        check_vma=False,
    )
```

profile of v0, /device:TPU:8, one launch (start us, length us, event | category | flops | bytes accessed | tf_op | source)
XLA Modules:
  0.0 226.9 jit_solution(2305887054889296009)
XLA Ops:
  10.5 4.6 %collective-permute-start = (bf16[2,384,384]{2,1,0:T(8,128)(2,1)S(1)}, bf16[2,384,384]{2,1,0:T(8,128)(2,1)S(1)}, u32[]{:S(2)}, u32[]{:S(2)}) collective-permute-start(bf16[2,384,384]{2,1,0:T(8,128)(2,1)S(1)} %constant_dynamic-update-slice_fusion), channel_id=1, source_target_pairs={{0,8},{8,16},{16,24},{24,32},{32,40},{40,48},{48,56},{1,9},{9,17},... | collective-permute-start | bytes 1769480 | tf_op jit(solution)/shard_map/ppermute | solution.py:33
  15.1 1.4 copy.25
  16.4 1.7 broadcast_in_dim.59
  18.1 6.8 %all-to-all-start = ((bf16[4,384,768]{1,2,0:T(8,128)(2,1)}), bf16[4,384,768]{1,2,0:T(8,128)(2,1)}, u32[]{:S(2)}, u32[]{:S(2)}) async-start(bf16[4,384,768]{1,2,0:T(8,128)(2,1)} %broadcast_in_dim.59), calls=%async_computation | async-start | bytes 4718592 | tf_op jit(solution)/shard_map/all_to_all | solution.py:18
  27.5 2.0 fusion.62
  38.0 1.3 fusion.33
  39.3 20.1 %all-to-all-done = bf16[4,384,768]{1,2,0:T(8,128)(2,1)} async-done(((bf16[4,384,768]{1,2,0:T(8,128)(2,1)}), bf16[4,384,768]{1,2,0:T(8,128)(2,1)}, u32[]{:S(2)}, u32[]{:S(2)}) %all-to-all-start) | async-done | bytes 2359328 | tf_op jit(solution)/shard_map/all_to_all | solution.py:18
  59.4 13.0 %all-gather.3.cloned.1.call-done = bf16[1,384,3072]{2,1,0:T(8,128)(2,1)} async-done(((bf16[1,384,384]{2,1,0:T(8,128)(2,1)}), bf16[1,384,3072]{2,1,0:T(8,128)(2,1)}) %all-gather.3.cloned.1.call-update) | async-done | bytes 2359312 | tf_op jit(solution)/shard_map/all_gather | solution.py:111
  72.4 4.0 %fusion.22 = bf16[384,384]{0,1:T(8,128)(2,1)S(1)} fusion(bf16[384,3072]{0,1:T(8,128)(2,1)} %bitcast.12, bf16[1,384,3072]{2,1,0:T(8,128)(2,1)} %all-gather.3.cloned.1.call-done, f32[3072]{0:T(1024)S(1)} %bitcast.122), kind=kOutput, calls=%fused_computation.38 | convolution fusion | flops 909656064 | bytes 5025792 | tf_op jit(solution)/shard_map/dot_general | solution.py:115
  76.9 1.3 fusion.56
  78.2 1.3 fusion.59
  81.0 1.6 fusion.11
  82.9 1.6 fusion.12
  84.5 2.2 convolution_multiply_fusion.3
  86.7 1.4 convolution_convert_fusion
  88.1 2.5 %copy.29 = bf16[384,3072]{0,1:T(8,128)(2,1)} copy(bf16[384,3072]{1,0:T(8,128)(2,1)S(1)} %convolution_convert_fusion) | data formatting | bytes 4718592 | tf_op jit(solution)/shard_map/convert_element_type | solution.py:165
  90.6 7.6 %all-to-all-start.1 = ((bf16[32,384,96]{1,2,0:T(8,128)(2,1)}), bf16[32,384,96]{1,2,0:T(8,128)(2,1)S(1)}, u32[]{:S(2)}, u32[]{:S(2)}) async-start(bf16[32,384,96]{1,2,0:T(8,128)(2,1)} %bitcast.112), calls=%async_computation.1 | async-start | bytes 4718592 | tf_op jit(solution)/shard_map/all_to_all | solution.py:56
  98.2 1.5 fusion.76
  103.4 4.2 %collective-permute-start.3 = (bf16[2,384,384]{1,2,0:T(8,128)(2,1)}, bf16[2,384,384]{1,2,0:T(8,128)(2,1)}, u32[]{:S(2)}, u32[]{:S(2)}) collective-permute-start(bf16[2,384,384]{1,2,0:T(8,128)(2,1)} %pad_maximum_fusion.4), channel_id=1, source_target_pairs={{0,8},{8,16},{16,24},{24,32},{32,40},{40,48},{48,56},{1,9},{9,17},... | collective-permute-start | bytes 1769480 | tf_op jit(solution)/shard_map/ppermute | solution.py:45
  111.2 1.8 fusion.28
  113.0 1.5 pad_maximum_fusion.1
  114.5 14.4 %all-to-all-done.1 = bf16[32,384,96]{1,2,0:T(8,128)(2,1)S(1)} async-done(((bf16[32,384,96]{1,2,0:T(8,128)(2,1)}), bf16[32,384,96]{1,2,0:T(8,128)(2,1)S(1)}, u32[]{:S(2)}, u32[]{:S(2)}) %all-to-all-start.1) | async-done | bytes 2359328 | tf_op jit(solution)/shard_map/all_to_all | solution.py:56
  130.4 5.5 %all-to-all-start.2 = ((f32[8,384,96]{1,2,0:T(8,128)}), f32[8,384,96]{1,2,0:T(8,128)S(1)}, u32[]{:S(2)}, u32[]{:S(2)}) async-start(f32[8,384,96]{1,2,0:T(8,128)} %broadcast_in_dim.64), calls=%async_computation.2 | async-start | bytes 2359296 | tf_op jit(solution)/shard_map/all_to_all | solution.py:18
  135.9 1.9 fusion.29
  137.8 1.7 fusion.30
  140.3 1.8 copy.30
  142.1 1.5 pad_maximum_fusion
  143.6 66.0 %all-reduce.3.cloned.1.call-done = (bf16[1,256,384]{1,2,0:T(8,128)(2,1)}, bf16[1,256,384]{1,2,0:T(8,128)(2,1)}) async-done(((bf16[1,256,384]{1,2,0:T(8,128)(2,1)}, bf16[1,256,384]{1,2,0:T(8,128)(2,1)}), (bf16[1,256,384]{1,2,0:T(8,128)(2,1)}, bf16[1,256,384]{1,2,0:T(8,128)(2,1)})) %all-reduce.3.cloned.1.call-update) | async-done | bytes 393232 | tf_op jit(solution)/shard_map/psum | solution.py:159
  209.7 1.7 copy.33
  211.4 1.7 copy.34
  215.4 1.5 fusion.41
  218.7 1.4 copy.35
  (137 shorter events, 29.2 us)
Async XLA Ops:
  9.2 20.6 %collective-permute-start.1 = (bf16[2,384,384]{2,1,0:T(8,128)(2,1)S(1)}, bf16[2,384,384]{2,1,0:T(8,128)(2,1)S(1)}, u32[]{:S(2)}, u32[]{:S(2)}) collective-permute-start(bf16[2,384,384]{2,1,0:T(8,128)(2,1)S(1)} %constant_dynamic-update-slice_fusion), channel_id=1, source_target_pairs={{8,0},{16,8},{24,16},{32,24},{40,32},{48,40},{56,48},{9,1},{17,9},... | collective-permute-start | bytes 1769480 | tf_op jit(solution)/shard_map/ppermute | solution.py:35
  10.5 19.3 %collective-permute-start = (bf16[2,384,384]{2,1,0:T(8,128)(2,1)S(1)}, bf16[2,384,384]{2,1,0:T(8,128)(2,1)S(1)}, u32[]{:S(2)}, u32[]{:S(2)}) collective-permute-start(bf16[2,384,384]{2,1,0:T(8,128)(2,1)S(1)} %constant_dynamic-update-slice_fusion), channel_id=1, source_target_pairs={{0,8},{8,16},{16,24},{24,32},{32,40},{40,48},{48,56},{1,9},{9,17},... | collective-permute-start | bytes 1769480 | tf_op jit(solution)/shard_map/ppermute | solution.py:33
  18.1 8.2 %copy-start.36 = (s32[1,2]{1,0:T(1,128)S(1)}, s32[1,2]{1,0:T(1,128)}, u32[]{:S(2)}) copy-start(s32[1,2]{1,0:T(1,128)} %param.19) | copy-start | bytes 28
  18.1 8.8 %copy-start.38 = (s32[8,1]{0,1:T(1,128)S(1)}, s32[8,1]{0,1:T(1,128)}, u32[]{:S(2)}) copy-start(s32[8,1]{0,1:T(1,128)} %param.20) | copy-start | bytes 100
  18.1 11.4 %copy-start.35 = (bf16[1,3072]{1,0:T(2,128)(2,1)S(1)}, bf16[1,3072]{1,0:T(2,128)(2,1)}, u32[]{:S(2)}) copy-start(bf16[1,3072]{1,0:T(2,128)(2,1)} %param.17) | copy-start | bytes 18436
  18.1 11.6 %copy-start.29 = (bf16[1,256,384]{2,1,0:T(8,128)(2,1)S(1)}, bf16[1,256,384]{2,1,0:T(8,128)(2,1)}, u32[]{:S(2)}) copy-start(bf16[1,256,384]{2,1,0:T(8,128)(2,1)} %param.14) | copy-start | bytes 589828
  18.1 11.6 %copy-start.30 = (bf16[1,256,384]{2,1,0:T(8,128)(2,1)S(1)}, bf16[1,256,384]{2,1,0:T(8,128)(2,1)}, u32[]{:S(2)}) copy-start(bf16[1,256,384]{2,1,0:T(8,128)(2,1)} %param.15) | copy-start | bytes 589828
  18.1 41.3 %all-to-all-start = ((bf16[4,384,768]{1,2,0:T(8,128)(2,1)}), bf16[4,384,768]{1,2,0:T(8,128)(2,1)}, u32[]{:S(2)}, u32[]{:S(2)}) async-start(bf16[4,384,768]{1,2,0:T(8,128)(2,1)} %broadcast_in_dim.59), calls=%async_computation | async-start | bytes 4718592 | tf_op jit(solution)/shard_map/all_to_all | solution.py:18
  24.9 47.5 %all-gather.3.cloned.1.call-start = ((), (), s32[]{:S(2)}) async-start(), calls=%async_computation.3 | async-start | bytes 2654208 | tf_op jit(solution)/shard_map/all_gather | solution.py:111
  29.7 2.5 %copy-start.32 = (bf16[256,128]{1,0:T(8,128)(2,1)}, bf16[256,128]{1,0:T(8,128)(2,1)S(1)}, u32[]{:S(2)}) copy-start(bf16[256,128]{1,0:T(8,128)(2,1)S(1)} %get-tuple-element.40) | copy-start | bytes 196612
  29.8 6.2 %copy-start.33 = (bf16[256,128]{1,0:T(8,128)(2,1)}, bf16[256,128]{1,0:T(8,128)(2,1)S(1)}, u32[]{:S(2)}) copy-start(bf16[256,128]{1,0:T(8,128)(2,1)S(1)} %get-tuple-element.37) | copy-start | bytes 196612
  31.2 1.9 copy-start.20
  31.2 3.3 %copy-start.23 = (bf16[1152,128]{1,0:T(8,128)(2,1)}, bf16[1152,128]{1,0:T(8,128)(2,1)S(1)}, u32[]{:S(2)}) copy-start(bf16[1152,128]{1,0:T(8,128)(2,1)S(1)} %get-tuple-element.32) | copy-start | bytes 884740
  31.2 4.7 %copy-start.25 = (bf16[1152,128]{1,0:T(8,128)(2,1)}, bf16[1152,128]{1,0:T(8,128)(2,1)S(1)}, u32[]{:S(2)}) copy-start(bf16[1152,128]{1,0:T(8,128)(2,1)S(1)} %get-tuple-element.31) | copy-start | bytes 884740
  32.8 2.8 %copy-start.2 = (f32[384,1408]{0,1:T(8,128)}, f32[384,1408]{0,1:T(8,128)S(1)}, u32[]{:S(2)}) copy-start(f32[384,1408]{0,1:T(8,128)S(1)} %get-tuple-element.50) | copy-start | bytes 6488068
  33.7 4.3 %copy-start = (f32[384,1408]{0,1:T(8,128)}, f32[384,1408]{0,1:T(8,128)S(1)}, u32[]{:S(2)}) copy-start(f32[384,1408]{0,1:T(8,128)S(1)} %get-tuple-element.46) | copy-start | bytes 6488068
  72.4 4.0 %copy-start.16 = (bf16[384,1408]{0,1:T(8,128)(2,1)S(1)}, bf16[384,1408]{0,1:T(8,128)(2,1)}, u32[]{:S(2)}) copy-start(bf16[384,1408]{0,1:T(8,128)(2,1)} %copy-done.15) | copy-start | bytes 3244036
  72.4 4.4 %copy-start.14 = (bf16[384,1408]{0,1:T(8,128)(2,1)S(1)}, bf16[384,1408]{0,1:T(8,128)(2,1)}, u32[]{:S(2)}) copy-start(bf16[384,1408]{0,1:T(8,128)(2,1)} %copy-done.13) | copy-start | bytes 3244036
  76.9 2.6 %copy-start.22 = (bf16[1152,128]{1,0:T(8,128)(2,1)S(1)}, bf16[1152,128]{1,0:T(8,128)(2,1)}, u32[]{:S(2)}) copy-start(bf16[1152,128]{1,0:T(8,128)(2,1)} %get-tuple-element.33) | copy-start | bytes 884740
  76.9 2.6 %copy-start.39 = (bf16[384,128]{0,1:T(8,128)(2,1)S(1)}, bf16[384,128]{0,1:T(8,128)(2,1)}, u32[]{:S(2)}) copy-start(bf16[384,128]{0,1:T(8,128)(2,1)} %convolution_convert_fusion.2) | copy-start | bytes 294916
  76.9 2.6 %copy-start.40 = (bf16[384,128]{0,1:T(8,128)(2,1)S(1)}, bf16[384,128]{0,1:T(8,128)(2,1)}, u32[]{:S(2)}) copy-start(bf16[384,128]{0,1:T(8,128)(2,1)} %convolution_convert_fusion.1) | copy-start | bytes 294916
  78.2 1.9 copy-start.34
  80.7 3.8 %copy-start.19 = (bf16[384,1408]{0,1:T(8,128)(2,1)}, bf16[384,1408]{0,1:T(8,128)(2,1)S(1)}, u32[]{:S(2)}) copy-start(bf16[384,1408]{0,1:T(8,128)(2,1)S(1)} %fusion.10) | copy-start | bytes 3244036
  82.9 3.8 %copy-start.37 = (bf16[1,384,3072]{2,1,0:T(8,128)(2,1)S(1)}, bf16[1,384,3072]{2,1,0:T(8,128)(2,1)}, u32[]{:S(2)}) copy-start(bf16[1,384,3072]{2,1,0:T(8,128)(2,1)} %all-gather.3.cloned.1.call-done) | copy-start | bytes 7077892
  90.6 38.4 %all-to-all-start.1 = ((bf16[32,384,96]{1,2,0:T(8,128)(2,1)}), bf16[32,384,96]{1,2,0:T(8,128)(2,1)S(1)}, u32[]{:S(2)}, u32[]{:S(2)}) async-start(bf16[32,384,96]{1,2,0:T(8,128)(2,1)} %bitcast.112), calls=%async_computation.1 | async-start | bytes 4718592 | tf_op jit(solution)/shard_map/all_to_all | solution.py:56
  98.2 111.5 %all-reduce.3.cloned.1.call-start = ((), (), s32[]{:S(2)}) async-start(), calls=%async_computation.4 | async-start | bytes 786432 | tf_op jit(solution)/shard_map/psum | solution.py:159
  103.4 109.7 %collective-permute-start.3 = (bf16[2,384,384]{1,2,0:T(8,128)(2,1)}, bf16[2,384,384]{1,2,0:T(8,128)(2,1)}, u32[]{:S(2)}, u32[]{:S(2)}) collective-permute-start(bf16[2,384,384]{1,2,0:T(8,128)(2,1)} %pad_maximum_fusion.4), channel_id=1, source_target_pairs={{0,8},{8,16},{16,24},{24,32},{32,40},{40,48},{48,56},{1,9},{9,17},... | collective-permute-start | bytes 1769480 | tf_op jit(solution)/shard_map/ppermute | solution.py:45
  108.5 105.8 %collective-permute-start.2 = (bf16[2,384,384]{1,2,0:T(8,128)(2,1)}, bf16[2,384,384]{1,2,0:T(8,128)(2,1)}, u32[]{:S(2)}, u32[]{:S(2)}) collective-permute-start(bf16[2,384,384]{1,2,0:T(8,128)(2,1)} %pad_maximum_fusion.3), channel_id=1, source_target_pairs={{8,0},{16,8},{24,16},{32,24},{40,32},{48,40},{56,48},{9,1},{17,9},... | collective-permute-start | bytes 1769480 | tf_op jit(solution)/shard_map/ppermute | solution.py:45
  130.4 88.3 %all-to-all-start.2 = ((f32[8,384,96]{1,2,0:T(8,128)}), f32[8,384,96]{1,2,0:T(8,128)S(1)}, u32[]{:S(2)}, u32[]{:S(2)}) async-start(f32[8,384,96]{1,2,0:T(8,128)} %broadcast_in_dim.64), calls=%async_computation.2 | async-start | bytes 2359296 | tf_op jit(solution)/shard_map/all_to_all | solution.py:18
  135.9 6.2 %copy-start.7 = (f32[1408,128]{0,1:T(8,128)S(1)}, f32[1408,128]{0,1:T(8,128)}, u32[]{:S(2)}) copy-start(f32[1408,128]{0,1:T(8,128)} %convolution_multiply_fusion.3) | copy-start | bytes 2162692
  135.9 6.2 %copy-start.9 = (f32[1408,128]{0,1:T(8,128)S(1)}, f32[1408,128]{0,1:T(8,128)}, u32[]{:S(2)}) copy-start(f32[1408,128]{0,1:T(8,128)} %copy-done.8) | copy-start | bytes 2162692
  135.9 6.2 %copy-start.11 = (f32[1408,128]{0,1:T(8,128)S(1)}, f32[1408,128]{0,1:T(8,128)}, u32[]{:S(2)}) copy-start(f32[1408,128]{0,1:T(8,128)} %copy-done.10) | copy-start | bytes 2162692
  (18 other events, 26.5 us)
Sparse Core Ops, SparseCore 0:
  27.5 44.8 all-gather.2
  111.3 98.3 all-reduce.2
where the time goes:
time: 229 us; the launch traced here: 227 us
  waiting for transfers between devices  114 us (50%)
  starting transfers between devices  31.2 us (14%)
  matrix products  24.9 us (11%)
  local copies, waits for them, and re-layouts  24.4 us (11%)
  other arithmetic  16.9 us (7%)
  between operations  15.2 us (7%)
    psum x1, waiting for transfers between devices, per_device(): lax.psum(grad_k[3 * tok:].astype(jnp.bfloat16), 'sp').astype(jnp.float32)  66 us
    all_to_all x2, waiting for transfers between devices, from_everyone(): return lax.all_to_all(copies, axis, split_axis=0, concat_axis=0, tiled=True)  20.1 us
    all_to_all x1, waiting for transfers between devices, summed_on_arrival(): parts = lax.all_to_all(cut_along(shard, dim, count), axis, 0, 0, tiled=True)  14.4 us
    unnamed x90, local copies, waits for them, and re-layouts  14.2 us
    all_gather x1, waiting for transfers between devices, per_device(): full_grad = lax.all_gather(grad_out[0], 'tp', axis=1, tiled=True)  13 us
    all_to_all x2, starting transfers between devices, from_everyone(): return lax.all_to_all(copies, axis, split_axis=0, concat_axis=0, tiled=True)  12.2 us
    all_to_all x1, starting transfers between devices, summed_on_arrival(): parts = lax.all_to_all(cut_along(shard, dim, count), axis, 0, 0, tiled=True)  7.58 us
    ppermute x2, starting transfers between devices, shifted(): return lax.ppermute(block, axis, route)  5.46 us
  transfers between devices with their start and end apart: 9, of which 4 were waited for; matrix products, arithmetic and copies ran while one was open for 19% of the time, Pallas kernels for 0%

commit v1 on v0

v1 whole, which is shorter than its diff:
```python
import functools

import jax
import jax.numpy as jnp
from jax import lax
from jax.experimental import pallas as pl
from jax.experimental.pallas import tpu as pltpu
from jax.sharding import PartitionSpec as P

HD = 128
TILE = 384
TXT = 256
HEADS = 3
N_TP = 8
KEYS = 3 * TILE + TXT
R_TXT = TILE
R_NEAR = (TILE + TXT, 2 * TILE + TXT)
QS = 3 * TILE
FAR = 1e30
MESH = pl.DeviceIdType.MESH
F32 = jnp.float32
BF16 = jnp.bfloat16


def dot(a, b, ca, cb):
    return lax.dot_general(a, b, (((ca,), (cb,)), ((), ())), preferred_element_type=F32)


def body(
    q_in, k_in, v_in, tk_in, tv_in, g_in, gate_in, w_in, win, tmap, tcount,
    o_q, o_k, o_v, o_tk, o_tv, o_w,
    qc, kc, vc, graw, sbuf, wbuf, scores, probs, pnear, att, d_out, acc, d_near,
    st_out, st_in, dl_out, dl_in, dl_own, ds_keep,
    gbuf, g_d, g_a, g_y, g_r, g_r1, g_r2, g_hs, g_rh, g_fin,
    tx, t_r1, t_r2, t_hs, t_rh, t_fin,
    loc, zs, zr, hs_s, hs_r, qs_s, qs_r, ss_s, ss_r, do_s, do_r, ws, wr,
    ds_, dr_, ys, yr, gs, gr, ts, tr,
):
    factor = HD ** (-0.5)
    dp = lax.axis_index("dp")
    sp = lax.axis_index("sp")
    tp = lax.axis_index("tp")
    core = dp % 2
    ylo = dp // 2
    yhi = sp // 4
    x = sp % 4
    y = yhi * 2 + ylo

    def at_xy(xx, yy, cc):
        return ((yy % 2) * 2 + cc, (yy // 2) * 4 + xx, tp)

    z_dev = (
        (dp, sp, (tp + 1) % N_TP),
        (dp, sp, (tp + N_TP - 1) % N_TP),
    )
    partner = ((ylo * 2 + 1 - core), sp, tp)
    y_next = at_xy(x, (y + 1) % 4, core)
    y_prev = at_xy(x, (y + 3) % 4, core)
    p1 = (dp, yhi * 4 + x + 1 - 2 * (x % 2), tp)
    p2 = (dp, yhi * 4 + (x + 3 + 2 * (x % 2)) % 4, tp)
    across = (dp, (1 - yhi) * 4 + x, tp)
    near_dev = ((dp, jnp.maximum(sp - 1, 0), tp), (dp, jnp.minimum(sp + 1, 7), tp))
    has = (sp > 0, sp < 7)

    def rc(src, dst, s_sem, r_sem, dev):
        return pltpu.make_async_remote_copy(
            src_ref=src, dst_ref=dst, send_sem=s_sem, recv_sem=r_sem,
            device_id=dev, device_id_type=MESH,
        )

    barrier = pltpu.get_barrier_semaphore()
    for dev in (z_dev[0], z_dev[1], partner, y_next, y_prev, p1, p2, across):
        pl.semaphore_signal(barrier, inc=1, device_id=dev, device_id_type=MESH)

    @pl.when(sp == 3)
    def _():
        pl.semaphore_signal(barrier, inc=1, device_id=near_dev[1], device_id_type=MESH)

    @pl.when(sp == 4)
    def _():
        pl.semaphore_signal(barrier, inc=1, device_id=near_dev[0], device_id_type=MESH)

    gcopy = pltpu.make_async_copy(g_in, graw, loc.at[0])
    gcopy.start()
    wcopy = pltpu.make_async_copy(w_in, wbuf.at[dp], loc.at[1])
    wcopy.start()
    kcopies, qcopies, vcopies = [], [], []
    for h in range(HEADS):
        cols = slice(h * HD, (h + 1) * HD)
        kcopies.append(pltpu.make_async_copy(k_in.at[:, cols], kc.at[h, 0:TILE], loc.at[2 + h]))
        vcopies.append(pltpu.make_async_copy(v_in.at[:, cols], vc.at[h, 0:TILE], loc.at[5 + h]))
        qcopies.append(pltpu.make_async_copy(q_in.at[:, cols], qc.at[h, 0:TILE], loc.at[8 + h]))
        kcopies.append(
            pltpu.make_async_copy(tk_in.at[:, cols], kc.at[h, R_TXT : R_TXT + TXT], loc.at[11 + h])
        )
        vcopies.append(
            pltpu.make_async_copy(tv_in.at[:, cols], vc.at[h, R_TXT : R_TXT + TXT], loc.at[14 + h])
        )
    for copy in kcopies + vcopies + qcopies:
        copy.start()

    for n in range(2):

        @pl.when(jnp.logical_not(has[n]))
        def _():
            rows = slice(R_NEAR[n], R_NEAR[n] + TILE)
            qrows = slice(TILE * (n + 1), TILE * (n + 2))
            for h in range(HEADS):
                kc[h, rows, :] = jnp.zeros((TILE, HD), BF16)
                vc[h, rows, :] = jnp.zeros((TILE, HD), BF16)
                qc[h, qrows, :] = jnp.zeros((TILE, HD), BF16)
            d_near[n] = jnp.zeros((TILE, TILE), BF16)
            st_in[n] = jnp.full((8, TILE), FAR, F32)
            dl_in[n] = jnp.zeros((8, TILE), F32)

    gcopy.wait()
    gate_own = gate_in[:, pl.ds(pl.multiple_of(tp * TILE, 128), TILE)].astype(F32)
    sbuf[tp] = (graw[...].astype(F32) * gate_own).astype(BF16)

    n_extra = jnp.where((sp == 3) | (sp == 4), 1, 0)
    pl.semaphore_wait(barrier, 8 + n_extra)

    def z_unit(k, u, d):
        step = 1 - 2 * d
        chunk = (tp + N_TP - step * k) % N_TP
        ref = sbuf.at[chunk, pl.ds(u * 192, 192), :]
        return rc(ref, ref, zs.at[d, k, u], zr.at[d, k, u], z_dev[d])

    def z_wait(k, u, d):
        step = 1 - 2 * d
        chunk = (tp + N_TP - step * (k + 1)) % N_TP
        ref = sbuf.at[chunk, pl.ds(u * 192, 192), :]
        rc(ref, ref, zs.at[d, k, u], zr.at[d, k, u], z_dev[d]).wait_recv()

    for u in range(2):
        for d in range(2):
            z_unit(0, u, d).start()

    def z_service(k):
        for u in range(2):
            for d in range(2):
                z_wait(k - 1, u, d)
                if u == d:
                    z_unit(k, u, d).start()
                else:

                    @pl.when(k < 3)
                    def _():
                        z_unit(k, u, d).start()

    for copy in kcopies + vcopies:
        copy.wait()

    def halo(h, n, which, mine):
        src = (kc, vc)[which]
        slot = R_NEAR[1 - n] if mine else R_NEAR[n]
        return rc(
            src.at[h, 0:TILE], src.at[h, pl.ds(slot, TILE)],
            hs_s.at[n, h, which], hs_r.at[1 - n if mine else n, h, which], near_dev[n],
        )

    def q_halo(n, mine):
        slot = TILE * (2 - n) if mine else TILE * (1 + n)
        return rc(
            qc.at[:, pl.ds(0, TILE)], qc.at[:, pl.ds(slot, TILE)],
            qs_s.at[n], qs_r.at[1 - n if mine else n], near_dev[n],
        )

    for copy in qcopies:
        copy.wait()
    wcopy.wait()
    w_part = rc(wbuf.at[dp], wbuf.at[dp], ws.at[0], wr.at[0], partner)
    w_next = rc(wbuf.at[dp, 0:192], wbuf.at[dp, 0:192], ws.at[1], wr.at[1], y_next)
    w_prev = rc(wbuf.at[dp, 192:384], wbuf.at[dp, 192:384], ws.at[2], wr.at[2], y_prev)
    w_next.start()
    w_prev.start()
    w_part.start()
    for n in range(2):

        @pl.when(has[n])
        def _():
            for h in range(HEADS):
                halo(h, n, 0, True).start()
                halo(h, n, 1, True).start()
            q_halo(n, True).start()

    own_pos = tmap[sp, 0]
    bias = []
    for n in range(2):
        other = tmap[(jnp.maximum(sp - 1, 0), jnp.minimum(sp + 1, 7))[n], 0]
        seen = (win[0, 0] >= 1) & (jnp.abs(own_pos - other) <= win[0, 1]) & has[n]
        bias.append(jnp.where(seen, 0.0, -FAR).astype(F32))
    text_rows = lax.broadcasted_iota(jnp.int32, (TXT, 1), 0)
    text_bias = jnp.where(text_rows < tcount[0], 0.0, -FAR).astype(F32)

    def early(h, carry):
        queries = qc[h, 0:TILE, :]
        own = factor * dot(kc[h, 0:TILE, :], queries, 1, 1)
        scores[h, 0:TILE, :] = own
        text = factor * dot(kc[h, R_TXT : R_TXT + TXT, :], queries, 1, 1) + text_bias
        scores[h, R_TXT : R_TXT + TXT, :] = text
        return carry

    lax.fori_loop(0, HEADS, early, 0)

    other = (1 - ylo) * 2 + core
    w_fwd = []
    for half in range(2):
        rows = slice(half * 192, half * 192 + 192)
        ref = wbuf.at[other, rows]
        rc(ref, ref, ws.at[1 + half], wr.at[1 + half], y_next).wait_recv()
        fwd = rc(ref, ref, ws.at[3 + half], wr.at[3 + half], partner)
        fwd.start()
        w_fwd.append(fwd)
    mate = ylo * 2 + 1 - core
    mate_other = (1 - ylo) * 2 + 1 - core
    rc(wbuf.at[mate], wbuf.at[mate], ws.at[0], wr.at[0], partner).wait_recv()
    for half in range(2):
        ref = wbuf.at[mate_other, half * 192 : half * 192 + 192]
        rc(ref, ref, ws.at[3 + half], wr.at[3 + half], partner).wait_recv()

    def take(chunk):
        cols = pl.ds(pl.multiple_of((chunk % 2) * TILE, 128), TILE)
        return dot(wbuf[chunk // 2, :, cols], sbuf[chunk], 1, 1)

    acc[...] = take(tp)

    def forward(h, carry):
        queries = qc[h, 0:TILE, :]
        for n in range(2):

            @pl.when(has[n])
            def _():
                halo(h, n, 0, False).wait_recv()
                halo(h, n, 1, False).wait_recv()

            rows = slice(R_NEAR[n], R_NEAR[n] + TILE)
            scores[h, rows, :] = factor * dot(kc[h, rows, :], queries, 1, 1) + bias[n]
        top = jnp.max(scores[h], axis=0, keepdims=True)
        weights = jnp.exp(scores[h] - top)
        inv = 1.0 / jnp.sum(weights, axis=0, keepdims=True)
        probs[h] = (weights * inv).astype(BF16)
        for n in range(2):
            st_out[n, pl.ds(h, 1), :] = jnp.where(bias[n] < 0.0, FAR, top)
            st_out[n, pl.ds(h + 4, 1), :] = inv
        att[h] = dot(vc[h], probs[h], 0, 0).astype(BF16)
        z_service(h + 1)
        acc[...] += take((tp + h + 1) % N_TP) + take((tp + N_TP - h - 1) % N_TP)
        return carry

    lax.fori_loop(0, HEADS, forward, 0)

    def st_copy(n, mine):
        return rc(
            st_out.at[n], st_in.at[1 - n if mine else n],
            ss_s.at[n], ss_r.at[1 - n if mine else n], near_dev[n],
        )

    for n in range(2):

        @pl.when(has[n])
        def _():
            st_copy(n, True).start()

    def grad_w(chunk):
        full = dot(att[...].reshape(HEADS * HD, TILE), sbuf[chunk], 1, 0)
        cols = pl.ds(pl.multiple_of((chunk % 2) * TILE, 128), TILE)
        gbuf[chunk // 2, :, cols] = full.astype(BF16)

    def grad_w_step(i, carry):
        grad_w((tp + i + 5) % N_TP)
        return carry

    lax.fori_loop(0, 7, grad_w_step, 0)

    for n in range(2):

        @pl.when(has[n])
        def _():
            q_halo(n, False).wait_recv()
            st_copy(n, False).wait_recv()

        def near_probs(h, carry):
            s = factor * dot(kc[h, 0:TILE, :], qc[h, TILE * (n + 1) : TILE * (n + 2), :], 1, 1)
            p = jnp.exp(s - st_in[n, pl.ds(h, 1), :]) * st_in[n, pl.ds(h + 4, 1), :]
            pnear[n, h] = p.astype(BF16)
            return carry

        lax.fori_loop(0, HEADS, near_probs, 0)

    z_wait(3, 0, 0)
    z_wait(3, 1, 1)
    last = (tp + 4) % N_TP
    total = acc[...] + take(last)
    d_out[...] = total.astype(BF16)
    dl_out[...] = jnp.zeros((8, TILE), F32)
    for h in range(HEADS):
        both = d_out[h * HD : (h + 1) * HD, :].astype(F32) * att[h].astype(F32)
        dl_out[h : h + 1, :] = jnp.sum(both, axis=0, keepdims=True)

    def do_copy(n, mine, which):
        to = 1 - n if mine else n
        src, dst = ((d_out, d_near.at[to]), (dl_out, dl_in.at[to]))[which]
        return rc(src, dst, do_s.at[n, which], do_r.at[to, which], near_dev[n])

    for n in range(2):

        @pl.when(has[n])
        def _():
            do_copy(n, True, 1).start()
            do_copy(n, True, 0).start()

    grad_w(last)

    def d_copy(i, src_core):
        return rc(gbuf.at[i * 2 + 1 - core], g_d.at[i], ds_.at[i], dr_.at[i], partner)

    for i in range(2):
        d_copy(i, core).start()

    def backward(h, carry):
        lanes = pl.ds(pl.multiple_of(h * HD, 128), HD)
        grads = d_out[pl.ds(pl.multiple_of(h * HD, 128), HD), :]
        delta = dl_out[pl.ds(h, 1), :]
        g = dot(vc[h], grads, 1, 0)
        ds = (probs[h].astype(F32) * (g - delta)).astype(BF16)
        ds_keep[h] = ds[0:TILE, :]
        gq = factor * dot(kc[h], ds, 0, 0)
        o_q[:, lanes] = gq.T.astype(BF16)
        trows = slice(R_TXT, R_TXT + TXT)
        tx[0:TXT, lanes] = (factor * dot(ds[trows, :], qc[h, 0:TILE, :], 1, 0)).astype(BF16)
        tx[TXT : 2 * TXT, lanes] = dot(probs[h, trows, :], grads, 1, 1).astype(BF16)
        return carry

    lax.fori_loop(0, HEADS, backward, 0)

    g1 = (x % 2 + x // 2) % 2
    g2 = x // 2

    def summer(src, fin, r1, r2, hs, rh, s_sem, r_sem):
        rows = src.shape[0]
        part, half, quarter = rows // 2, rows // 4, rows // 8

        def at(ref, start, size):
            return ref.at[pl.ds(pl.multiple_of(start, 16), size), :]

        def rd(ref, start, size):
            return ref[pl.ds(pl.multiple_of(start, 16), size), :].astype(F32)

        a1, b1 = g1 * half, part + g2 * half
        a2, b2 = a1 + g2 * quarter, b1 + g1 * quarter
        na1, nb1 = (1 - g1) * half, part + (1 - g2) * half
        na2, nb2 = a1 + (1 - g2) * quarter, b1 + (1 - g1) * quarter
        copies = [
            (rc(at(src, na1, half), r1.at[0:half], s_sem.at[0], r_sem.at[0], p1),
             rc(at(src, nb1, half), r1.at[half : 2 * half], s_sem.at[1], r_sem.at[1], p2)),
            (rc(at(src, na2, quarter), r2.at[0:quarter], s_sem.at[2], r_sem.at[2], p2),
             rc(at(src, nb2, quarter), r2.at[quarter : 2 * quarter], s_sem.at[3], r_sem.at[3], p1)),
            (rc(hs, rh, s_sem.at[4], r_sem.at[4], across),),
            (rc(at(fin, a2, quarter), at(fin, a2, quarter), s_sem.at[5], r_sem.at[5], p2),
             rc(at(fin, b2, quarter), at(fin, b2, quarter), s_sem.at[6], r_sem.at[6], p1)),
            (rc(at(fin, a1, half), at(fin, a1, half), s_sem.at[7], r_sem.at[7], p1),
             rc(at(fin, b1, half), at(fin, b1, half), s_sem.at[8], r_sem.at[8], p2)),
        ]
        arrive = [
            (rc(at(fin, na2, quarter), at(fin, na2, quarter), s_sem.at[5], r_sem.at[5], p2),
             rc(at(fin, nb2, quarter), at(fin, nb2, quarter), s_sem.at[6], r_sem.at[6], p1)),
            (rc(at(fin, na1, half), at(fin, na1, half), s_sem.at[7], r_sem.at[7], p1),
             rc(at(fin, nb1, half), at(fin, nb1, half), s_sem.at[8], r_sem.at[8], p2)),
        ]

        def go(stage):
            if stage == 1:
                for c in copies[0]:
                    c.wait_recv()
                for start, low in ((a1, 0), (b1, half)):
                    at(src, start, half)[...] = (
                        rd(src, start, half) + r1[low : low + half, :].astype(F32)
                    ).astype(BF16)
            elif stage == 2:
                for c in copies[1]:
                    c.wait_recv()
                for start, low in ((a2, 0), (b2, quarter)):
                    hs[low : low + quarter, :] = (
                        rd(src, start, quarter) + r2[low : low + quarter, :].astype(F32)
                    ).astype(BF16)
            elif stage == 3:
                copies[2][0].wait_recv()
                for start, low in ((a2, 0), (b2, quarter)):
                    at(fin, start, quarter)[...] = (
                        hs[low : low + quarter, :].astype(F32)
                        + rh[low : low + quarter, :].astype(F32)
                    ).astype(BF16)
            elif stage >= 4:
                for c in arrive[stage - 4]:
                    c.wait_recv()
            if stage < 5:
                for c in copies[stage]:
                    c.start()
            else:
                for group in copies:
                    for c in group:
                        c.wait_send()

        return go

    t_go = summer(tx, t_fin, t_r1, t_r2, t_hs, t_rh, ts, tr)
    t_go(0)

    for i in range(2):
        d_copy(i, core).wait_recv()
    g_a[...] = (gbuf[(1 - ylo) * 2 + core].astype(F32) + g_d[1 - ylo].astype(F32)).astype(BF16)
    y_sends = [
        rc(g_a.at[0:192], g_y.at[0:192], ys.at[0], yr.at[0], y_next),
        rc(g_a.at[192:384], g_y.at[192:384], ys.at[1], yr.at[1], y_prev),
    ]
    for c in y_sends:
        c.start()
    g_r[...] = (gbuf[ylo * 2 + core].astype(F32) + g_d[ylo].astype(F32)).astype(BF16)

    t_go(1)
    for c in y_sends:
        c.wait_recv()
    g_r[...] = (g_r[...].astype(F32) + g_y[...].astype(F32)).astype(BF16)
    g_go = summer(g_r, g_fin, g_r1, g_r2, g_hs, g_rh, gs, gr)
    g_go(0)
    t_go(2)

    for n in range(2):

        @pl.when(has[n])
        def _():
            do_copy(n, False, 1).wait_recv()
            do_copy(n, False, 0).wait_recv()

    def own_keys(h, carry):
        lanes = pl.ds(pl.multiple_of(h * HD, 128), HD)
        hrows = pl.ds(pl.multiple_of(h * HD, 128), HD)
        gk = dot(ds_keep[h], qc[h, 0:TILE, :], 1, 0)
        gv = dot(probs[h, 0:TILE, :], d_out[hrows, :], 1, 1)
        for n in range(2):
            grads = d_near[n, hrows, :]
            p = pnear[n, h]
            g = dot(vc[h, 0:TILE, :], grads, 1, 0)
            ds = (p.astype(F32) * (g - dl_in[n, pl.ds(h, 1), :])).astype(BF16)
            gk += dot(ds, qc[h, TILE * (n + 1) : TILE * (n + 2), :], 1, 0)
            gv += dot(p, grads, 1, 1)
        o_k[:, lanes] = (factor * gk).astype(BF16)
        o_v[:, lanes] = gv.astype(BF16)
        return carry

    lax.fori_loop(0, HEADS, own_keys, 0)

    g_go(1)
    t_go(3)
    g_go(2)
    t_go(4)
    g_go(3)
    t_go(5)
    o_tk[...] = t_fin[0:TXT, :]
    o_tv[...] = t_fin[TXT : 2 * TXT, :]
    g_go(4)
    g_go(5)
    o_w[...] = g_fin[...].astype(F32)

    for d in range(2):
        for k in range(4):
            for u in range(2):
                if k < 3 or u == d:
                    z_unit(k, u, d).wait_send()
    for c in (w_part, w_next, w_prev, *w_fwd, *y_sends):
        c.wait_send()
    for i in range(2):
        d_copy(i, core).wait_send()
    for n in range(2):

        @pl.when(has[n])
        def _():
            for h in range(HEADS):
                halo(h, n, 0, True).wait_send()
                halo(h, n, 1, True).wait_send()
            q_halo(n, True).wait_send()
            st_copy(n, True).wait_send()
            do_copy(n, True, 0).wait_send()
            do_copy(n, True, 1).wait_send()


def per_device(
    query, key, value, text_key, text_value, grad_out, gate, out_weight, windows, tile_map, text_count
):
    anyspec = pl.BlockSpec(memory_space=pl.ANY)
    vmem = pl.BlockSpec(memory_space=pltpu.VMEM)
    smem = pl.BlockSpec(memory_space=pltpu.SMEM)
    sds = jax.ShapeDtypeStruct
    v = pltpu.VMEM
    dma = pltpu.SemaphoreType.DMA
    out = pl.pallas_call(
        body,
        out_shape=(
            sds((TILE, TILE), BF16),
            sds((TILE, TILE), BF16),
            sds((TILE, TILE), BF16),
            sds((TXT, TILE), BF16),
            sds((TXT, TILE), BF16),
            sds((TILE, 768), F32),
        ),
        in_specs=[anyspec] * 6 + [vmem, anyspec] + [smem] * 3,
        out_specs=(vmem,) * 6,
        scratch_shapes=[
            v((HEADS, QS, HD), BF16),
            v((HEADS, KEYS, HD), BF16),
            v((HEADS, KEYS, HD), BF16),
            v((TILE, TILE), BF16),
            v((N_TP, TILE, TILE), BF16),
            v((4, TILE, 768), BF16),
            v((HEADS, KEYS, TILE), F32),
            v((HEADS, KEYS, TILE), BF16),
            v((2, HEADS, TILE, TILE), BF16),
            v((HEADS, HD, TILE), BF16),
            v((TILE, TILE), BF16),
            v((TILE, TILE), F32),
            v((2, TILE, TILE), BF16),
            v((2, 8, TILE), F32),
            v((2, 8, TILE), F32),
            v((8, TILE), F32),
            v((2, 8, TILE), F32),
            v((8, TILE), F32),
            v((HEADS, TILE, TILE), BF16),
            v((4, TILE, 768), BF16),
            v((2, TILE, 768), BF16),
            v((TILE, 768), BF16),
            v((TILE, 768), BF16),
            v((TILE, 768), BF16),
            v((192, 768), BF16),
            v((96, 768), BF16),
            v((96, 768), BF16),
            v((96, 768), BF16),
            v((TILE, 768), BF16),
            v((2 * TXT, TILE), BF16),
            v((TXT, TILE), BF16),
            v((TXT // 2, TILE), BF16),
            v((TXT // 2, TILE), BF16),
            v((TXT // 2, TILE), BF16),
            v((2 * TXT, TILE), BF16),
            dma((17,)),
            dma((2, 4, 2)),
            dma((2, 4, 2)),
            dma((2, HEADS, 2)),
            dma((2, HEADS, 2)),
            dma((2,)),
            dma((2,)),
            dma((2,)),
            dma((2,)),
            dma((2, 2)),
            dma((2, 2)),
            dma((5,)),
            dma((5,)),
            dma((2,)),
            dma((2,)),
            dma((2,)),
            dma((2,)),
            dma((9,)),
            dma((9,)),
            dma((9,)),
            dma((9,)),
        ],
        compiler_params=pltpu.CompilerParams(
            collective_id=0, has_side_effects=True, vmem_limit_bytes=60 * 1024 * 1024
        ),
    )(
        query[0], key[0], value[0], text_key[0], text_value[0], grad_out[0], gate, out_weight,
        windows, tile_map, text_count,
    )
    return tuple(o[None] for o in out[:5]) + (out[5],)


def solution(mesh):
    placed = (
        P("dp", "sp", "tp"),
        P("dp", "sp", "tp"),
        P("dp", "sp", "tp"),
        P("dp", None, "tp"),
        P("dp", None, "tp"),
        P("dp", "sp", "tp"),
        P("dp", None),
        P("tp", "dp"),
        P("sp", None),
        P(),
        P("dp"),
    )
    return jax.shard_map(
        per_device,
        mesh=mesh,
        in_specs=placed,
        out_specs=(
            P("dp", "sp", "tp"),
            P("dp", "sp", "tp"),
            P("dp", "sp", "tp"),
            P("dp", None, "tp"),
            P("dp", None, "tp"),
            P("tp", "dp"),
        ),
        check_vma=False,
    )
```

time: 229 us -> 113 us (0.49)
  waiting for transfers between devices: 114 us -> 0 us
  Pallas kernels: 0 us -> 102 us
  starting transfers between devices: 31.2 us -> 0 us
  matrix products: 24.9 us -> 0 us
  other arithmetic: 16.9 us -> 0 us
  local copies, waits for them, and re-layouts: 24.4 us -> 7.96 us
  between operations: 15.2 us -> 1.32 us
    pallas_call x0 -> x1, Pallas kernels: none -> 102 us  [per_device(): pl.pallas_call(body, out_shape=(sds((TILE, TILE), BF16), sds((TILE, TILE)...]
    psum x1 -> x0, waiting for transfers between devices: 66 us -> none  [per_device(): lax.psum(grad_k[3 * tok:].astype(jnp.bfloat16), 'sp').astype(jnp.float32)]
    all_to_all x3 -> x0, waiting for transfers between devices: 34.5 us -> none  [the longest x2 20.1 us: from_everyone(): return lax.all_to_all(copies, axis, split_axis=0, concat_axis=0, tiled=True)]
    dot_general x20 -> x0, matrix products: 24.9 us -> none  [the longest x3 5.36 us: tile_attention(): jnp.dot(grad_scores, keys, preferred_element_type=jnp.float32)]
    all_to_all x3 -> x0, starting transfers between devices: 19.8 us -> none  [the longest x2 12.2 us: from_everyone(): return lax.all_to_all(copies, axis, split_axis=0, concat_axis=0, tiled=True)]
    all_gather x1 -> x0, waiting for transfers between devices: 13 us -> none  [per_device(): full_grad = lax.all_gather(grad_out[0], 'tp', axis=1, tiled=True)]
    ppermute x4 -> x0, starting transfers between devices: 11.3 us -> none  [the longest x2 5.46 us: shifted(): return lax.ppermute(block, axis, route)]
    unnamed x90 -> x15, local copies, waits for them, and re-layouts: 14.2 us -> 7.96 us
  transfers between devices with their start and end apart: 9 -> 0, of which waited for: 4 -> 0; matrix products, arithmetic and copies ran while one was open for 19% -> 0% of each run, Pallas kernels for 0% -> 0%
where the time goes in v1:
time: 113 us; the launch traced here: 111 us
  Pallas kernels  102 us (90%)
  local copies, waits for them, and re-layouts  7.96 us (7%)
  between operations  1.32 us (1%)
    pallas_call x1, Pallas kernels, per_device(): pl.pallas_call(body, out_shape=(sds((TILE, TILE), BF16), sds((TILE, TILE)...  102 us
    unnamed x15, local copies, waits for them, and re-layouts  7.96 us

profile of v1, /device:TPU:8, one launch (start us, length us, event | category | flops | bytes accessed | tf_op | source)
XLA Modules:
  0.0 111.3 jit_solution(15786117226437149048)
XLA Ops:
  1.3 1.3 %copy.17.tmap = s32[8,1]{1,0:T(8,128)} copy(s32[8,1]{0,1:T(1,128)} %param.20) | data formatting | bytes 64 | tf_op args[9]
  2.6 102.0 %shard_map.154 = (bf16[384,384]{1,0:T(8,128)(2,1)}, bf16[384,384]{1,0:T(8,128)(2,1)}, bf16[384,384]{1,0:T(8,128)(2,1)}, bf16[256,384]{1,0:T(8,128)(2,1)}, bf16[256,384]{1,0:T(8,128)(2,1)}, /*index=5*/f32[384,768]{1,0:T(8,128)}) custom-call(bf16[384,384]{1,0:T(8,128)(2,1)} %bitcast.14, bf16[384,384]{1,0:T(8,128)(2,1)} %bitcast.15, bf16[384,384]{1,0:T(8,128)(2,1)} %bitcast.16, ...), custom_call_target="tpu_custom_call" | custom-call | tf_op jit(solution)/shard_map/pallas_call | solution.py:497
  104.6 0.0 copy-start.1
  104.7 0.0 copy-start.3
  104.7 0.0 copy-start.2
  104.7 0.0 copy-start
  104.7 1.8 %copy.25 = bf16[1,384,384]{2,1,0:T(8,128)(2,1)} copy(bf16[1,384,384]{2,1,0:T(8,128)(2,1)} %bitcast.13) | data formatting | bytes 589824
  106.5 1.7 %copy.26 = bf16[1,384,384]{2,1,0:T(8,128)(2,1)} copy(bf16[1,384,384]{2,1,0:T(8,128)(2,1)} %bitcast.12) | data formatting | bytes 589824
  108.2 0.0 copy-done.1
  108.2 0.7 copy.27
  108.9 0.0 copy-done.3
  108.9 0.7 copy.28
  109.6 0.0 copy-done.2
  109.6 0.7 copy.29
  110.3 0.0 copy-done
  110.3 1.0 copy.30
Async XLA Ops:
  104.6 3.6 %copy-start.1 = (bf16[384,384]{1,0:T(8,128)(2,1)S(1)}, bf16[384,384]{1,0:T(8,128)(2,1)}, u32[]{:S(2)}) copy-start(bf16[384,384]{1,0:T(8,128)(2,1)} %get-tuple-element.14) | copy-start | bytes 884740
  104.7 4.3 %copy-start.3 = (bf16[256,384]{1,0:T(8,128)(2,1)S(1)}, bf16[256,384]{1,0:T(8,128)(2,1)}, u32[]{:S(2)}) copy-start(bf16[256,384]{1,0:T(8,128)(2,1)} %get-tuple-element.15) | copy-start | bytes 589828
  104.7 5.0 %copy-start.2 = (bf16[256,384]{1,0:T(8,128)(2,1)S(1)}, bf16[256,384]{1,0:T(8,128)(2,1)}, u32[]{:S(2)}) copy-start(bf16[256,384]{1,0:T(8,128)(2,1)} %get-tuple-element.16) | copy-start | bytes 589828
  104.7 5.6 %copy-start = (f32[384,768]{1,0:T(8,128)S(1)}, f32[384,768]{1,0:T(8,128)}, u32[]{:S(2)}) copy-start(f32[384,768]{1,0:T(8,128)} %get-tuple-element.29) | copy-start | bytes 3538948

commit v2 on v1

--- a/solution.py
+++ b/solution.py
@@ -33,8 +33,8 @@
     st_out, st_in, dl_out, dl_in, dl_own, ds_keep,
     gbuf, g_d, g_a, g_y, g_r, g_r1, g_r2, g_hs, g_rh, g_fin,
     tx, t_r1, t_r2, t_hs, t_rh, t_fin,
-    loc, zs, zr, hs_s, hs_r, qs_s, qs_r, ss_s, ss_r, do_s, do_r, ws, wr,
-    ds_, dr_, ys, yr, gs, gr, ts, tr,
+    rbuf, dbuf, loc, zs, zr, hs_s, hs_r, qs_s, qs_r, ss_s, ss_r, do_s, do_r, ws, wr,
+    ds_, dr_, ys, yr, gs, gr, ts, tr, rs_s, rs_r, rf_s, rf_r, rd_s, rd_r, rg_s, rg_r,
 ):
     factor = HD ** (-0.5)
     dp = lax.axis_index("dp")
@@ -72,13 +72,28 @@
     for dev in (z_dev[0], z_dev[1], partner, y_next, y_prev, p1, p2, across):
         pl.semaphore_signal(barrier, inc=1, device_id=dev, device_id_type=MESH)
 
-    @pl.when(sp == 3)
+    other = (1 - ylo) * 2 + core
+    end = (sp == 3) | (sp == 4)
+    relay = (x == 0) | (x == 3)
+    to_later = (x == 0).astype(jnp.int32)
+    relay_from = (other, 4 - to_later, tp)
+    relay_to = (other, 3 + to_later, tp)
+    relay_half = (yhi + 2 - ylo - to_later) % 2
+    relays = []
+    for half in range(2):
+        mid = (half + ylo + jnp.where(sp == 3, 0, 1)) % 2
+        relays.append((other, mid * 4 + jnp.where(sp == 3, 0, 3), tp))
+    from_side = jnp.where(sp == 4, 0, 1)
+
+    @pl.when(end)
     def _():
-        pl.semaphore_signal(barrier, inc=1, device_id=near_dev[1], device_id_type=MESH)
-
-    @pl.when(sp == 4)
+        for dev in ((other, 0, tp), (other, 3, tp), (other, 4, tp), (other, 7, tp), (dp, jnp.where(sp == 3, 4, 3), tp)):
+            pl.semaphore_signal(barrier, inc=1, device_id=dev, device_id_type=MESH)
+
+    @pl.when(relay)
     def _():
-        pl.semaphore_signal(barrier, inc=1, device_id=near_dev[0], device_id_type=MESH)
+        for dev in ((other, 3, tp), (other, 4, tp)):
+            pl.semaphore_signal(barrier, inc=1, device_id=dev, device_id_type=MESH)
 
     gcopy = pltpu.make_async_copy(g_in, graw, loc.at[0])
     gcopy.start()
@@ -117,7 +132,7 @@
     gate_own = gate_in[:, pl.ds(pl.multiple_of(tp * TILE, 128), TILE)].astype(F32)
     sbuf[tp] = (graw[...].astype(F32) * gate_own).astype(BF16)
 
-    n_extra = jnp.where((sp == 3) | (sp == 4), 1, 0)
+    n_extra = jnp.where(end, 5, 0) + jnp.where(relay, 2, 0)
     pl.semaphore_wait(barrier, 8 + n_extra)
 
     def z_unit(k, u, d):
@@ -140,13 +155,8 @@
         for u in range(2):
             for d in range(2):
                 z_wait(k - 1, u, d)
-                if u == d:
+                if k < 3 or u == d:
                     z_unit(k, u, d).start()
-                else:
-
-                    @pl.when(k < 3)
-                    def _():
-                        z_unit(k, u, d).start()
 
     for copy in kcopies + vcopies:
         copy.wait()
@@ -175,21 +185,63 @@
     w_next.start()
     w_prev.start()
     w_part.start()
+    def side(n):
+        return (sp == 4) if n == 0 else (sp == 3)
+
+    plain = tuple(has[n] & jnp.logical_not(side(n)) for n in range(2))
+
+    def piece_src(piece):
+        if piece < 6:
+            return (kc, vc)[piece % 2].at[piece // 2]
+        return qc.at[piece - 6]
+
+    def end_send(piece, half):
+        rows = slice(half * 192, half * 192 + 192)
+        return rc(
+            piece_src(piece).at[rows], rbuf.at[piece],
+            rs_s.at[half, piece], rs_r.at[piece], relays[half],
+        )
+
+    def forward_piece(piece):
+        base = R_NEAR[0] if piece < 6 else TILE
+        start = base + (1 - to_later) * TILE + relay_half * 192
+        dst = piece_src(piece).at[pl.ds(pl.multiple_of(start, 16), 192), :]
+        return rc(rbuf.at[piece], dst, rf_s.at[piece], rf_r.at[relay_half, piece], relay_to)
+
+    def relay_pieces(pieces):
+        @pl.when(relay)
+        def _():
+            for piece in pieces:
+                rc(rbuf.at[piece], rbuf.at[piece], rf_s.at[piece], rs_r.at[piece], relay_from).wait_recv()
+                forward_piece(piece).start()
+
+    def end_wait(piece):
+        for half in range(2):
+            start = (R_NEAR[0] if piece < 6 else TILE) + from_side * TILE + half * 192
+            dst = piece_src(piece).at[pl.ds(pl.multiple_of(start, 16), 192), :]
+            rc(dst, dst, rf_s.at[piece], rf_r.at[half, piece], relays[half]).wait_recv()
+
+    @pl.when(end)
+    def _():
+        for piece in range(9):
+            for half in range(2):
+                end_send(piece, half).start()
+
     for n in range(2):
 
-        @pl.when(has[n])
+        @pl.when(plain[n])
         def _():
             for h in range(HEADS):
                 halo(h, n, 0, True).start()
                 halo(h, n, 1, True).start()
             q_halo(n, True).start()
 
-    own_pos = tmap[sp, 0]
+    own_pos = tmap[pl.ds(sp, 1), :]
     bias = []
     for n in range(2):
-        other = tmap[(jnp.maximum(sp - 1, 0), jnp.minimum(sp + 1, 7))[n], 0]
-        seen = (win[0, 0] >= 1) & (jnp.abs(own_pos - other) <= win[0, 1]) & has[n]
-        bias.append(jnp.where(seen, 0.0, -FAR).astype(F32))
+        near_pos = tmap[pl.ds((jnp.maximum(sp - 1, 0), jnp.minimum(sp + 1, 7))[n], 1), :]
+        reach = jnp.where((win[0, 0] >= 1) & has[n], win[0, 1], -1)
+        bias.append(jnp.where(jnp.abs(own_pos - near_pos) <= reach, 0.0, -FAR).astype(F32))
     text_rows = lax.broadcasted_iota(jnp.int32, (TXT, 1), 0)
     text_bias = jnp.where(text_rows < tcount[0], 0.0, -FAR).astype(F32)
 
@@ -203,7 +255,41 @@
 
     lax.fori_loop(0, HEADS, early, 0)
 
-    other = (1 - ylo) * 2 + core
+    def take(chunk):
+        cols = pl.ds(pl.multiple_of((chunk % 2) * TILE, 128), TILE)
+        return dot(wbuf[chunk // 2, :, cols], sbuf[chunk], 1, 1)
+
+    def forward(h):
+        queries = qc[h, 0:TILE, :]
+        for n in range(2):
+
+            @pl.when(plain[n])
+            def _():
+                halo(h, n, 0, False).wait_recv()
+                halo(h, n, 1, False).wait_recv()
+
+        @pl.when(end)
+        def _():
+            end_wait(2 * h)
+            end_wait(2 * h + 1)
+
+        for n in range(2):
+            rows = slice(R_NEAR[n], R_NEAR[n] + TILE)
+            scores[h, rows, :] = factor * dot(kc[h, rows, :], queries, 1, 1) + bias[n]
+        top = jnp.max(scores[h], axis=0, keepdims=True)
+        weights = jnp.exp(scores[h] - top)
+        inv = 1.0 / jnp.sum(weights, axis=0, keepdims=True)
+        probs[h] = (weights * inv).astype(BF16)
+        for n in range(2):
+            st_out[n, h : h + 1, :] = jnp.where(bias[n] < 0.0, FAR, top)
+            st_out[n, h + 4 : h + 5, :] = inv
+        att[h] = dot(vc[h], probs[h], 0, 0).astype(BF16)
+
+    relay_pieces((0, 1))
+    z_service(1)
+    forward(0)
+    relay_pieces((2, 3))
+    forward(1)
     w_fwd = []
     for half in range(2):
         rows = slice(half * 192, half * 192 + 192)
@@ -212,6 +298,21 @@
         fwd = rc(ref, ref, ws.at[3 + half], wr.at[3 + half], partner)
         fwd.start()
         w_fwd.append(fwd)
+    z_service(2)
+    relay_pieces((4, 5))
+    forward(2)
+    def st_copy(n, mine):
+        return rc(
+            st_out.at[n], st_in.at[1 - n if mine else n],
+            ss_s.at[n], ss_r.at[1 - n if mine else n], near_dev[n],
+        )
+
+    for n in range(2):
+
+        @pl.when(has[n])
+        def _():
+            st_copy(n, True).start()
+
     mate = ylo * 2 + 1 - core
     mate_other = (1 - ylo) * 2 + 1 - core
     rc(wbuf.at[mate], wbuf.at[mate], ws.at[0], wr.at[0], partner).wait_recv()
@@ -219,48 +320,13 @@
         ref = wbuf.at[mate_other, half * 192 : half * 192 + 192]
         rc(ref, ref, ws.at[3 + half], wr.at[3 + half], partner).wait_recv()
 
-    def take(chunk):
-        cols = pl.ds(pl.multiple_of((chunk % 2) * TILE, 128), TILE)
-        return dot(wbuf[chunk // 2, :, cols], sbuf[chunk], 1, 1)
-
     acc[...] = take(tp)
 
-    def forward(h, carry):
-        queries = qc[h, 0:TILE, :]
-        for n in range(2):
-
-            @pl.when(has[n])
-            def _():
-                halo(h, n, 0, False).wait_recv()
-                halo(h, n, 1, False).wait_recv()
-
-            rows = slice(R_NEAR[n], R_NEAR[n] + TILE)
-            scores[h, rows, :] = factor * dot(kc[h, rows, :], queries, 1, 1) + bias[n]
-        top = jnp.max(scores[h], axis=0, keepdims=True)
-        weights = jnp.exp(scores[h] - top)
-        inv = 1.0 / jnp.sum(weights, axis=0, keepdims=True)
-        probs[h] = (weights * inv).astype(BF16)
-        for n in range(2):
-            st_out[n, pl.ds(h, 1), :] = jnp.where(bias[n] < 0.0, FAR, top)
-            st_out[n, pl.ds(h + 4, 1), :] = inv
-        att[h] = dot(vc[h], probs[h], 0, 0).astype(BF16)
-        z_service(h + 1)
+    def more(h, carry):
         acc[...] += take((tp + h + 1) % N_TP) + take((tp + N_TP - h - 1) % N_TP)
         return carry
 
-    lax.fori_loop(0, HEADS, forward, 0)
-
-    def st_copy(n, mine):
-        return rc(
-            st_out.at[n], st_in.at[1 - n if mine else n],
-            ss_s.at[n], ss_r.at[1 - n if mine else n], near_dev[n],
-        )
-
-    for n in range(2):
-
-        @pl.when(has[n])
-        def _():
-            st_copy(n, True).start()
+    lax.fori_loop(0, 2, more, 0)
 
     def grad_w(chunk):
         full = dot(att[...].reshape(HEADS * HD, TILE), sbuf[chunk], 1, 0)
@@ -271,13 +337,26 @@
         grad_w((tp + i + 5) % N_TP)
         return carry
 
-    lax.fori_loop(0, 7, grad_w_step, 0)
+    lax.fori_loop(1, 6, grad_w_step, 0)
+    relay_pieces((6, 7, 8))
+    z_service(3)
+    more(2, 0)
+    grad_w((tp + 5) % N_TP)
+    grad_w((tp + 3) % N_TP)
 
     for n in range(2):
 
+        @pl.when(plain[n])
+        def _():
+            q_halo(n, False).wait_recv()
+
+        @pl.when(side(n))
+        def _():
+            for piece in (6, 7, 8):
+                end_wait(piece)
+
         @pl.when(has[n])
         def _():
-            q_halo(n, False).wait_recv()
             st_copy(n, False).wait_recv()
 
         def near_probs(h, carry):
@@ -303,11 +382,45 @@
         src, dst = ((d_out, d_near.at[to]), (dl_out, dl_in.at[to]))[which]
         return rc(src, dst, do_s.at[n, which], do_r.at[to, which], near_dev[n])
 
+    half_rows = HD // 2
+
+    def end_grad(h, half):
+        rows = slice(h * HD + half * half_rows, h * HD + (half + 1) * half_rows)
+        return rc(d_out.at[rows], dbuf.at[h], rd_s.at[half, h], rd_r.at[h], relays[half])
+
+    def forward_grad(h):
+        rows = pl.ds(pl.multiple_of(h * HD + relay_half * half_rows, 16), half_rows)
+        dst = d_near.at[1 - to_later, rows, :]
+        return rc(dbuf.at[h], dst, rg_s.at[h], rg_r.at[relay_half, h], relay_to)
+
+    def relay_grads():
+        @pl.when(relay)
+        def _():
+            for h in range(HEADS):
+                rc(dbuf.at[h], dbuf.at[h], rg_s.at[h], rd_r.at[h], relay_from).wait_recv()
+                forward_grad(h).start()
+
+    def end_grad_wait():
+        for h in range(HEADS):
+            for half in range(2):
+                rows = slice(h * HD + half * half_rows, h * HD + (half + 1) * half_rows)
+                dst = d_near.at[from_side, rows, :]
+                rc(dst, dst, rg_s.at[h], rg_r.at[half, h], relays[half]).wait_recv()
+
+    @pl.when(end)
+    def _():
+        for h in range(HEADS):
+            for half in range(2):
+                end_grad(h, half).start()
+
     for n in range(2):
 
         @pl.when(has[n])
         def _():
             do_copy(n, True, 1).start()
+
+        @pl.when(plain[n])
+        def _():
             do_copy(n, True, 0).start()
 
     grad_w(last)
@@ -407,6 +520,7 @@
     t_go = summer(tx, t_fin, t_r1, t_r2, t_hs, t_rh, ts, tr)
     t_go(0)
 
+    relay_grads()
     for i in range(2):
         d_copy(i, core).wait_recv()
     g_a[...] = (gbuf[(1 - ylo) * 2 + core].astype(F32) + g_d[1 - ylo].astype(F32)).astype(BF16)
@@ -431,7 +545,14 @@
         @pl.when(has[n])
         def _():
             do_copy(n, False, 1).wait_recv()
+
+        @pl.when(plain[n])
+        def _():
             do_copy(n, False, 0).wait_recv()
+
+    @pl.when(end)
+    def _():
+        end_grad_wait()
 
     def own_keys(h, carry):
         lanes = pl.ds(pl.multiple_of(h * HD, 128), HD)
@@ -461,7 +582,7 @@
     o_tv[...] = t_fin[TXT : 2 * TXT, :]
     g_go(4)
     g_go(5)
-    o_w[...] = g_fin[...].astype(F32)
+    o_w[...] = g_fin[...]
 
     for d in range(2):
         for k in range(4):
@@ -474,15 +595,46 @@
         d_copy(i, core).wait_send()
     for n in range(2):
 
-        @pl.when(has[n])
+        @pl.when(plain[n])
         def _():
             for h in range(HEADS):
                 halo(h, n, 0, True).wait_send()
                 halo(h, n, 1, True).wait_send()
             q_halo(n, True).wait_send()
+            do_copy(n, True, 0).wait_send()
+
+        @pl.when(has[n])
+        def _():
             st_copy(n, True).wait_send()
-            do_copy(n, True, 0).wait_send()
             do_copy(n, True, 1).wait_send()
+
+    @pl.when(end)
+    def _():
+        for half in range(2):
+            for piece in range(9):
+                end_send(piece, half).wait_send()
+            for h in range(HEADS):
+                end_grad(h, half).wait_send()
+
+    @pl.when(relay)
+    def _():
+        for piece in range(9):
+            forward_piece(piece).wait_send()
+        for h in range(HEADS):
+            forward_grad(h).wait_send()
+
+
+def finish(*refs):
+    given, results, wide, sems = refs[:6], refs[6:12], refs[12], refs[13]
+    copies = []
+    for i in range(5):
+        copies.append(pltpu.make_async_copy(given[i], results[i].at[0], sems.at[i]))
+        copies[-1].start()
+    wide[...] = given[5][...].astype(F32)
+    copies.append(pltpu.make_async_copy(wide, results[5], sems.at[5]))
+    copies[-1].start()
+    for copy in copies:
+        copy.wait()
 
 
 def per_device(
@@ -502,9 +654,9 @@
             sds((TILE, TILE), BF16),
             sds((TXT, TILE), BF16),
             sds((TXT, TILE), BF16),
-            sds((TILE, 768), F32),
+            sds((TILE, 768), BF16),
         ),
-        in_specs=[anyspec] * 6 + [vmem, anyspec] + [smem] * 3,
+        in_specs=[anyspec] * 6 + [vmem, anyspec, smem, vmem, smem],
         out_specs=(vmem,) * 6,
         scratch_shapes=[
             v((HEADS, QS, HD), BF16),
@@ -542,6 +694,8 @@
             v((TXT // 2, TILE), BF16),
             v((TXT // 2, TILE), BF16),
             v((2 * TXT, TILE), BF16),
+            v((9, 192, HD), BF16),
+            v((HEADS, HD // 2, TILE), BF16),
             dma((17,)),
             dma((2, 4, 2)),
             dma((2, 4, 2)),
@@ -563,6 +717,14 @@
             dma((9,)),
             dma((9,)),
             dma((9,)),
+            dma((2, 9)),
+            dma((9,)),
+            dma((9,)),
+            dma((2, 9)),
+            dma((2, HEADS)),
+            dma((HEADS,)),
+            dma((HEADS,)),
+            dma((2, HEADS)),
         ],
         compiler_params=pltpu.CompilerParams(
             collective_id=0, has_side_effects=True, vmem_limit_bytes=60 * 1024 * 1024
@@ -571,7 +733,20 @@
         query[0], key[0], value[0], text_key[0], text_value[0], grad_out[0], gate, out_weight,
         windows, tile_map, text_count,
     )
-    return tuple(o[None] for o in out[:5]) + (out[5],)
+    return pl.pallas_call(
+        finish,
+        out_shape=(
+            sds((1, TILE, TILE), BF16),
+            sds((1, TILE, TILE), BF16),
+            sds((1, TILE, TILE), BF16),
+            sds((1, TXT, TILE), BF16),
+            sds((1, TXT, TILE), BF16),
+            sds((TILE, 768), F32),
+        ),
+        in_specs=[vmem] * 6,
+        out_specs=(anyspec,) * 6,
+        scratch_shapes=[v((TILE, 768), F32), dma((6,))],
+    )(*out)
 
 
 def solution(mesh):

time: 113 us -> 95.4 us (0.84); the launches traced: 111 us -> 95.2 us
  Pallas kernels: 102 us -> 92.6 us
  local copies, waits for them, and re-layouts: 7.96 us -> 1.32 us
    pallas_call x1, Pallas kernels: 102 us -> 89.6 us  [per_device(): pl.pallas_call(body, out_shape=(sds((TILE, TILE), BF16), sds((TILE, TILE)...]
    unnamed x15 -> x1, local copies, waits for them, and re-layouts: 7.96 us -> 1.32 us
    pallas_call x0 -> x1, Pallas kernels: none -> 2.98 us  [per_device(): pl.pallas_call(finish, out_shape=(sds((1, TILE, TILE), BF16), sds((1, TIL...]
where the time goes in v2:
time: 95.4 us; the launch traced here: 95.2 us
  Pallas kernels  92.6 us (97%)
  local copies, waits for them, and re-layouts  1.32 us (1%)
  between operations  1.29 us (1%)
    pallas_call x1, Pallas kernels, per_device(): pl.pallas_call(body, out_shape=(sds((TILE, TILE), BF16), sds((TILE, TILE)...  89.6 us
    pallas_call x1, Pallas kernels, per_device(): pl.pallas_call(finish, out_shape=(sds((1, TILE, TILE), BF16), sds((1, TIL...  2.98 us

profile of v2, /device:TPU:8, one launch (start us, length us, event | category | flops | bytes accessed | tf_op | source)
XLA Modules:
  0.0 95.2 jit_solution(11265663251101628321)
XLA Ops:
  1.3 1.3 %copy.17.tmap = s32[8,1]{1,0:T(8,128)} copy(s32[8,1]{0,1:T(1,128)} %param.20) | data formatting | bytes 64 | tf_op args[9]
  2.6 89.6 %shard_map.154 = (bf16[384,384]{1,0:T(8,128)(2,1)}, bf16[384,384]{1,0:T(8,128)(2,1)}, bf16[384,384]{1,0:T(8,128)(2,1)}, bf16[256,384]{1,0:T(8,128)(2,1)}, bf16[2...) custom-call(bf16[384,384]{1,0:T(8,128)(2,1)} %bitcast.6, bf16[384,384]{1,0:T(8,128)(2,1)} %bitcast.7, ...), custom_call_target="tpu_custom_call" | custom-call | tf_op jit(solution)/shard_map/pallas_call | solution.py:649
  92.2 3.0 %shard_map.155 = (bf16[1,384,384]{2,1,0:T(8,128)(2,1)}, bf16[1,384,384]{2,1,0:T(8,128)(2,1)}, bf16[1,384,384]{2,1,0:T(8,128)(2,1)}, bf16[1,256,384]{2,1,0:T(8,12...) custom-call(bf16[384,384]{1,0:T(8,128)(2,1)} %get-tuple-element.12.refs_0_, ...), custom_call_target="tpu_custom_call" | custom-call | tf_op jit(solution)/shard_map/pallas_call | solution.py:736

commit v3 on v2

v3 whole, which is shorter than its diff:
```python
import functools

import jax
import jax.numpy as jnp
from jax import lax
from jax.experimental import pallas as pl
from jax.experimental.pallas import tpu as pltpu
from jax.sharding import PartitionSpec as P

HD = 128
TILE = 384
TXT = 256
HEADS = 3
N_TP = 8
KEYS = 3 * TILE + TXT
R_TXT = TILE
R_NEAR = (TILE + TXT, 2 * TILE + TXT)
QS = 3 * TILE
FAR = 1e30
MESH = pl.DeviceIdType.MESH
F32 = jnp.float32
BF16 = jnp.bfloat16


def dot(a, b, ca, cb):
    return lax.dot_general(a, b, (((ca,), (cb,)), ((), ())), preferred_element_type=F32)


def body(
    q_in, k_in, v_in, tk_in, tv_in, g_in, gate_in, w_in, win, tmap, tcount,
    o_q, o_k, o_v, o_tk, o_tv, o_w,
    qc, kc, vc, graw, sbuf, wbuf, scores, probs, pnear, att, d_out, acc, d_near,
    st_out, st_in, dl_out, dl_in, dl_own, ds_keep,
    gbuf, g_d, g_a, g_y, g_r, g_r1, g_r2, g_hs, g_rh, g_fin,
    tx, t_r1, t_r2, t_hs, t_rh, t_fin,
    gate_ref, q_acc, k_acc, v_acc, rbuf, dbuf, loc, zs, zr, hs_s, hs_r, qs_s, qs_r, ss_s, ss_r, do_s, do_r, ws, wr,
    ds_, dr_, ys, yr, gs, gr, ts, tr, rs_s, rs_r, rf_s, rf_r, rd_s, rd_r, rg_s, rg_r,
):
    factor = HD ** (-0.5)
    dp = lax.axis_index("dp")
    sp = lax.axis_index("sp")
    tp = lax.axis_index("tp")
    core = dp % 2
    ylo = dp // 2
    yhi = sp // 4
    x = sp % 4
    y = yhi * 2 + ylo

    def at_xy(xx, yy, cc):
        return ((yy % 2) * 2 + cc, (yy // 2) * 4 + xx, tp)

    z_dev = (
        (dp, sp, (tp + 1) % N_TP),
        (dp, sp, (tp + N_TP - 1) % N_TP),
    )
    partner = ((ylo * 2 + 1 - core), sp, tp)
    y_next = at_xy(x, (y + 1) % 4, core)
    y_prev = at_xy(x, (y + 3) % 4, core)
    p1 = (dp, yhi * 4 + x + 1 - 2 * (x % 2), tp)
    p2 = (dp, yhi * 4 + (x + 3 + 2 * (x % 2)) % 4, tp)
    across = (dp, (1 - yhi) * 4 + x, tp)
    near_dev = ((dp, jnp.maximum(sp - 1, 0), tp), (dp, jnp.minimum(sp + 1, 7), tp))
    has = (sp > 0, sp < 7)

    def rc(src, dst, s_sem, r_sem, dev):
        return pltpu.make_async_remote_copy(
            src_ref=src, dst_ref=dst, send_sem=s_sem, recv_sem=r_sem,
            device_id=dev, device_id_type=MESH,
        )

    barrier = pltpu.get_barrier_semaphore()
    for dev in (z_dev[0], z_dev[1], partner, y_next, y_prev, p1, p2, across):
        pl.semaphore_signal(barrier, inc=1, device_id=dev, device_id_type=MESH)

    other = (1 - ylo) * 2 + core
    end = (sp == 3) | (sp == 4)
    relay = (sp == 0) | (sp == 7)
    relays = ((other, 0, tp), (other, 7, tp))
    relay_to = ((other, 4, tp), (other, 3, tp))
    relay_half = sp // 7
    flow = jnp.where(sp == 3, 0, 1)
    from_side = 1 - flow

    @pl.when(end)
    def _():
        for dev in (*relays, (dp, jnp.where(sp == 3, 4, 3), tp)):
            pl.semaphore_signal(barrier, inc=1, device_id=dev, device_id_type=MESH)

    @pl.when(relay)
    def _():
        for dev in relay_to:
            pl.semaphore_signal(barrier, inc=1, device_id=dev, device_id_type=MESH)

    gcopy = pltpu.make_async_copy(g_in, graw, loc.at[0])
    gcopy.start()
    gate_copy = pltpu.make_async_copy(
        gate_in.at[:, pl.ds(pl.multiple_of(tp * TILE, 128), TILE)], gate_ref, loc.at[5]
    )
    gate_copy.start()
    wcopy = pltpu.make_async_copy(w_in, wbuf.at[dp], loc.at[1])
    wcopy.start()
    kcopies, qcopies, vcopies = [], [], []
    for h in range(HEADS):
        cols = slice(h * HD, (h + 1) * HD)
        kcopies.append(pltpu.make_async_copy(k_in.at[:, cols], kc.at[h, 0:TILE], loc.at[2]))
        vcopies.append(pltpu.make_async_copy(v_in.at[:, cols], vc.at[h, 0:TILE], loc.at[3]))
        qcopies.append(pltpu.make_async_copy(q_in.at[:, cols], qc.at[h, 0:TILE], loc.at[4]))
        kcopies.append(
            pltpu.make_async_copy(tk_in.at[:, cols], kc.at[h, R_TXT : R_TXT + TXT], loc.at[2])
        )
        vcopies.append(
            pltpu.make_async_copy(tv_in.at[:, cols], vc.at[h, R_TXT : R_TXT + TXT], loc.at[3])
        )
    for copy in kcopies + vcopies + qcopies:
        copy.start()

    for n in range(2):

        @pl.when(jnp.logical_not(has[n]))
        def _():
            rows = slice(R_NEAR[n], R_NEAR[n] + TILE)
            qrows = slice(TILE * (n + 1), TILE * (n + 2))
            for h in range(HEADS):
                kc[h, rows, :] = jnp.zeros((TILE, HD), BF16)
                vc[h, rows, :] = jnp.zeros((TILE, HD), BF16)
                qc[h, qrows, :] = jnp.zeros((TILE, HD), BF16)
            d_near[n] = jnp.zeros((TILE, TILE), BF16)
            st_in[n] = jnp.full((8, TILE), FAR, F32)
            dl_in[n] = jnp.zeros((8, TILE), F32)

    gcopy.wait()
    gate_copy.wait()
    gate_own = gate_ref[...].astype(F32)
    sbuf[tp] = (graw[...].astype(F32) * gate_own).astype(BF16)

    n_extra = jnp.where(end, 3, 0) + jnp.where(relay, 2, 0)
    pl.semaphore_wait(barrier, 8 + n_extra)

    def z_unit(k, u, d):
        step = 1 - 2 * d
        chunk = (tp + N_TP - step * k) % N_TP
        ref = sbuf.at[chunk, pl.ds(u * 192, 192), :]
        return rc(ref, ref, zs.at[d, k // 3], zr.at[d, k, u], z_dev[d])

    def z_wait(k, u, d):
        step = 1 - 2 * d
        chunk = (tp + N_TP - step * (k + 1)) % N_TP
        ref = sbuf.at[chunk, pl.ds(u * 192, 192), :]
        rc(ref, ref, zs.at[d, k // 3], zr.at[d, k, u], z_dev[d]).wait_recv()

    for u in range(2):
        for d in range(2):
            z_unit(0, u, d).start()

    def z_service(k, units=(0, 1)):
        for u in units:
            for d in range(2):
                z_wait(k - 1, u, d)
                if k < 3 or u == d:
                    z_unit(k, u, d).start()

    def drain(ref, sem):
        pltpu.make_async_copy(ref, ref, sem).wait()

    drain(kc.at[:, 0 : TILE + TXT], loc.at[2])
    drain(vc.at[:, 0 : TILE + TXT], loc.at[3])

    def halo(h, n, which, mine):
        src = (kc, vc)[which]
        slot = R_NEAR[1 - n] if mine else R_NEAR[n]
        return rc(
            src.at[h, 0:TILE], src.at[h, pl.ds(slot, TILE)],
            hs_s.at[n], hs_r.at[1 - n if mine else n, h], near_dev[n],
        )

    def q_halo(n, mine):
        slot = TILE * (2 - n) if mine else TILE * (1 + n)
        return rc(
            qc.at[:, pl.ds(0, TILE)], qc.at[:, pl.ds(slot, TILE)],
            qs_s.at[n], qs_r.at[1 - n if mine else n], near_dev[n],
        )

    drain(qc.at[:, 0:TILE], loc.at[4])
    wcopy.wait()
    w_part = rc(wbuf.at[dp], wbuf.at[dp], ws.at[0], wr.at[0], partner)
    w_next = rc(wbuf.at[dp, 0:192], wbuf.at[dp, 0:192], ws.at[1], wr.at[1], y_next)
    w_prev = rc(wbuf.at[dp, 192:384], wbuf.at[dp, 192:384], ws.at[2], wr.at[2], y_prev)
    def side(n):
        return (sp == 4) if n == 0 else (sp == 3)

    plain = tuple(has[n] & jnp.logical_not(side(n)) for n in range(2))

    def piece_src(piece):
        if piece < 6:
            return (kc, vc)[piece % 2].at[piece // 2]
        return qc.at[piece - 6]

    def end_send(piece, half):
        rows = slice(half * 192, half * 192 + 192)
        return rc(
            piece_src(piece).at[rows], rbuf.at[flow, piece],
            rs_s.at[half], rs_r.at[flow, min(piece // 2, 3)], relays[half],
        )

    def forward_piece(piece, f):
        start = (R_NEAR[0] if piece < 6 else TILE) + f * TILE + relay_half * 192
        dst = piece_src(piece).at[pl.ds(pl.multiple_of(start, 16), 192), :]
        return rc(rbuf.at[f, piece], dst, rf_s.at[f], rf_r.at[relay_half, min(piece // 2, 3)], relay_to[f])

    def relay_pieces(pieces):
        @pl.when(relay)
        def _():
            group = min(pieces[0] // 2, 3)
            for f in range(2):
                ref = rbuf.at[f, pieces[0] : pieces[-1] + 1]
                rc(ref, ref, rf_s.at[f], rs_r.at[f, group], relay_to[1 - f]).wait_recv()
                for piece in pieces:
                    forward_piece(piece, f).start()

    def end_wait(group):
        for half in range(2):
            ref = rbuf.at[0, 2 * group : 2 * group + (2 if group < 3 else 3)]
            rc(ref, ref, rf_s.at[0], rf_r.at[half, group], relays[half]).wait_recv()

    @pl.when(end)
    def _():
        for piece in range(9):
            for half in range(2):
                end_send(piece, half).start()

    for n in range(2):

        @pl.when(plain[n])
        def _():
            for h in range(HEADS):
                halo(h, n, 0, True).start()
                halo(h, n, 1, True).start()
            q_halo(n, True).start()

    own_pos = tmap[sp]
    bias = []
    for n in range(2):
        near_pos = tmap[(jnp.maximum(sp - 1, 0), jnp.minimum(sp + 1, 7))[n]]
        reach = jnp.where((win[0] >= 1) & has[n], win[1], -1)
        bias.append(jnp.where(jnp.abs(own_pos - near_pos) <= reach, 0.0, -FAR).astype(F32))
    text_rows = lax.broadcasted_iota(jnp.int32, (TXT, 1), 0)
    text_bias = jnp.where(text_rows < tcount[0], 0.0, -FAR).astype(F32)

    def early(h, carry):
        queries = qc[h, 0:TILE, :]
        own = factor * dot(kc[h, 0:TILE, :], queries, 1, 1)
        scores[h, 0:TILE, :] = own
        text = factor * dot(kc[h, R_TXT : R_TXT + TXT, :], queries, 1, 1) + text_bias
        scores[h, R_TXT : R_TXT + TXT, :] = text
        return carry

    lax.fori_loop(0, HEADS, early, 0)

    def take(chunk):
        cols = pl.ds(pl.multiple_of((chunk % 2) * TILE, 128), TILE)
        return dot(wbuf[chunk // 2, :, cols], sbuf[chunk], 1, 1)

    def forward(h):
        queries = qc[h, 0:TILE, :]
        for n in range(2):

            @pl.when(plain[n])
            def _():
                both = kc.at[0:2, 0:TILE]
                rc(both, both, hs_s.at[n], hs_r.at[n, h], near_dev[n]).wait_recv()

        @pl.when(end)
        def _():
            end_wait(h)

        for n in range(2):
            rows = slice(R_NEAR[n], R_NEAR[n] + TILE)
            scores[h, rows, :] = factor * dot(kc[h, rows, :], queries, 1, 1) + bias[n]
        top = jnp.max(scores[h], axis=0, keepdims=True)
        weights = jnp.exp(scores[h] - top)
        inv = 1.0 / jnp.sum(weights, axis=0, keepdims=True)
        probs[h] = (weights * inv).astype(BF16)
        for n in range(2):
            st_out[n, h : h + 1, :] = jnp.where(bias[n] < 0.0, FAR, top)
            st_out[n, h + 4 : h + 5, :] = inv
        att[h] = dot(vc[h], probs[h], 0, 0).astype(BF16)

    z_service(1, (0,))
    relay_pieces((0, 1))
    z_service(1, (1,))
    forward(0)
    relay_pieces((2, 3))
    w_next.start()
    w_prev.start()
    w_part.start()
    forward(1)
    relay_pieces((4, 5))
    z_service(2)
    forward(2)
    def st_copy(n, mine):
        return rc(
            st_out.at[n], st_in.at[1 - n if mine else n],
            ss_s.at[n], ss_r.at[1 - n if mine else n], near_dev[n],
        )

    for n in range(2):

        @pl.when(has[n])
        def _():
            st_copy(n, True).start()

    def grad_w(chunk):
        full = dot(att[...].reshape(HEADS * HD, TILE), sbuf[chunk], 1, 0)
        cols = pl.ds(pl.multiple_of((chunk % 2) * TILE, 128), TILE)
        gbuf[chunk // 2, :, cols] = full.astype(BF16)

    def grad_w_step(i, carry):
        grad_w((tp + i + 5) % N_TP)
        return carry

    g1 = (x % 2 + x // 2) % 2
    g2 = x // 2

    def summer(src, fin, r1, r2, hs, rh, s_sem, r_sem):
        rows = src.shape[0]
        part, half, quarter = rows // 2, rows // 4, rows // 8

        def at(ref, start, size):
            return ref.at[pl.ds(pl.multiple_of(start, 16), size), :]

        def rd(ref, start, size):
            return ref[pl.ds(pl.multiple_of(start, 16), size), :].astype(F32)

        a1, b1 = g1 * half, part + g2 * half
        a2, b2 = a1 + g2 * quarter, b1 + g1 * quarter
        na1, nb1 = (1 - g1) * half, part + (1 - g2) * half
        na2, nb2 = a1 + (1 - g2) * quarter, b1 + (1 - g1) * quarter
        copies = [
            (rc(at(src, na1, half), r1.at[0:half], s_sem.at[0], r_sem.at[0], p1),
             rc(at(src, nb1, half), r1.at[half : 2 * half], s_sem.at[1], r_sem.at[1], p2)),
            (rc(at(src, na2, quarter), r2.at[0:quarter], s_sem.at[2], r_sem.at[2], p2),
             rc(at(src, nb2, quarter), r2.at[quarter : 2 * quarter], s_sem.at[3], r_sem.at[3], p1)),
            (rc(hs, rh, s_sem.at[4], r_sem.at[4], across),),
            (rc(at(fin, a2, quarter), at(fin, a2, quarter), s_sem.at[5], r_sem.at[5], p2),
             rc(at(fin, b2, quarter), at(fin, b2, quarter), s_sem.at[6], r_sem.at[6], p1)),
            (rc(at(fin, a1, half), at(fin, a1, half), s_sem.at[7], r_sem.at[7], p1),
             rc(at(fin, b1, half), at(fin, b1, half), s_sem.at[8], r_sem.at[8], p2)),
        ]
        arrive = [
            (rc(at(fin, na2, quarter), at(fin, na2, quarter), s_sem.at[5], r_sem.at[5], p2),
             rc(at(fin, nb2, quarter), at(fin, nb2, quarter), s_sem.at[6], r_sem.at[6], p1)),
            (rc(at(fin, na1, half), at(fin, na1, half), s_sem.at[7], r_sem.at[7], p1),
             rc(at(fin, nb1, half), at(fin, nb1, half), s_sem.at[8], r_sem.at[8], p2)),
        ]

        def go(stage):
            if stage == 1:
                for c in copies[0]:
                    c.wait_recv()
                for start, low in ((a1, 0), (b1, half)):
                    at(src, start, half)[...] = (
                        rd(src, start, half) + r1[low : low + half, :].astype(F32)
                    ).astype(BF16)
            elif stage == 2:
                for c in copies[1]:
                    c.wait_recv()
                for start, low in ((a2, 0), (b2, quarter)):
                    hs[low : low + quarter, :] = (
                        rd(src, start, quarter) + r2[low : low + quarter, :].astype(F32)
                    ).astype(BF16)
            elif stage == 3:
                copies[2][0].wait_recv()
                for start, low in ((a2, 0), (b2, quarter)):
                    at(fin, start, quarter)[...] = (
                        hs[low : low + quarter, :].astype(F32)
                        + rh[low : low + quarter, :].astype(F32)
                    ).astype(BF16)
            elif stage >= 4:
                for c in arrive[stage - 4]:
                    c.wait_recv()
            if stage < 5:
                for c in copies[stage]:
                    c.start()
            else:
                for group in copies:
                    for c in group:
                        c.wait_send()

        return go

    g_go = summer(g_r, g_fin, g_r1, g_r2, g_hs, g_rh, gs, gr)
    t_go = summer(tx, t_fin, t_r1, t_r2, t_hs, t_rh, ts, tr)

    turn = 2 * (tp % 2) - 1
    blocks = tuple((tp // 2 + d + 4) % 4 for d in (0, turn, -turn, 2))

    def d_copy(i):
        b = blocks[i]
        return rc(gbuf.at[b], g_d.at[b // 2], ds_.at[i], dr_.at[i], partner)

    def d_send(i):
        @pl.when(blocks[i] % 2 != core)
        def _():
            d_copy(i).start()

    y_sends = [
        rc(g_a.at[0:192], g_y.at[0:192], ys.at[0], yr.at[0], y_next),
        rc(g_a.at[192:384], g_y.at[192:384], ys.at[1], yr.at[1], y_prev),
    ]

    def y_send(i):
        b = blocks[i]

        @pl.when(b % 2 == core)
        def _():
            d_copy(i).wait_recv()
            both = (gbuf[b].astype(F32) + g_d[b // 2].astype(F32)).astype(BF16)

            @pl.when(b != dp)
            def _():
                g_a[...] = both
                for c in y_sends:
                    c.start()

            @pl.when(b == dp)
            def _():
                g_r[...] = both

    def y_take(i):
        @pl.when(blocks[i] == dp)
        def _():
            for c in y_sends:
                c.wait_recv()
            g_r[...] = (g_r[...].astype(F32) + g_y[...].astype(F32)).astype(BF16)
            g_go(0)

    def g_early(stage):
        @pl.when(blocks[3] != dp)
        def _():
            g_go(stage)

    def g_late(stage):
        @pl.when(blocks[3] == dp)
        def _():
            g_go(stage)

    lax.fori_loop(2, 5, grad_w_step, 0)
    d_send(0)
    grad_w((tp + 6) % N_TP)
    grad_w((tp + 2) % N_TP)
    d_send(1)
    w_fwd = []
    for half in range(2):
        rows = slice(half * 192, half * 192 + 192)
        ref = wbuf.at[other, rows]
        rc(ref, ref, ws.at[1 + half], wr.at[1 + half], y_next).wait_recv()
        fwd = rc(ref, ref, ws.at[3 + half], wr.at[3 + half], partner)
        fwd.start()
        w_fwd.append(fwd)
    y_send(0)
    mate = ylo * 2 + 1 - core
    mate_other = (1 - ylo) * 2 + 1 - core
    rc(wbuf.at[mate], wbuf.at[mate], ws.at[0], wr.at[0], partner).wait_recv()
    for half in range(2):
        ref = wbuf.at[mate_other, half * 192 : half * 192 + 192]
        rc(ref, ref, ws.at[3 + half], wr.at[3 + half], partner).wait_recv()

    acc[...] = take(tp)

    def more(h, carry):
        acc[...] += take((tp + h + 1) % N_TP) + take((tp + N_TP - h - 1) % N_TP)
        return carry

    lax.fori_loop(0, 2, more, 0)

    relay_pieces((6, 7, 8))
    z_service(3)
    more(2, 0)
    grad_w((tp + 5) % N_TP)
    grad_w((tp + 3) % N_TP)
    d_send(2)
    y_send(1)

    for n in range(2):

        @pl.when(plain[n])
        def _():
            q_halo(n, False).wait_recv()

        @pl.when(side(n))
        def _():
            end_wait(3)

        @pl.when(has[n])
        def _():
            st_copy(n, False).wait_recv()

        def near_probs(h, carry):
            s = factor * dot(kc[h, 0:TILE, :], qc[h, TILE * (n + 1) : TILE * (n + 2), :], 1, 1)
            p = jnp.exp(s - st_in[n, pl.ds(h, 1), :]) * st_in[n, pl.ds(h + 4, 1), :]
            pnear[n, h] = p.astype(BF16)
            return carry

        lax.fori_loop(0, HEADS, near_probs, 0)

    y_send(2)
    y_take(0)
    y_take(1)
    z_wait(3, 0, 0)
    z_wait(3, 1, 1)
    last = (tp + 4) % N_TP
    total = acc[...] + take(last)
    d_out[...] = total.astype(BF16)
    dl_out[...] = jnp.zeros((8, TILE), F32)
    for h in range(HEADS):
        both = d_out[h * HD : (h + 1) * HD, :].astype(F32) * att[h].astype(F32)
        dl_out[h : h + 1, :] = jnp.sum(both, axis=0, keepdims=True)

    def do_copy(n, mine, which):
        to = 1 - n if mine else n
        src, dst = ((d_out, d_near.at[to]), (dl_out, dl_in.at[to]))[which]
        return rc(src, dst, do_s.at[n, which], do_r.at[to, which], near_dev[n])

    half_rows = HD // 2

    def end_grad(h, half):
        rows = slice(h * HD + half * half_rows, h * HD + (half + 1) * half_rows)
        return rc(
            d_out.at[rows], dbuf.at[flow, h], rd_s.at[half], rd_r.at[flow, h], relays[half]
        )

    def forward_grad(h, f):
        rows = pl.ds(pl.multiple_of(h * HD + relay_half * half_rows, 16), half_rows)
        return rc(
            dbuf.at[f, h], d_near.at[f, rows, :], rg_s.at[f], rg_r.at[relay_half], relay_to[f]
        )

    def relay_grads():
        @pl.when(relay)
        def _():
            for h in range(HEADS):
                for f in range(2):
                    ref = dbuf.at[f, h]
                    rc(ref, ref, rg_s.at[f], rd_r.at[f, h], relay_to[1 - f]).wait_recv()
                    forward_grad(h, f).start()

    def end_grad_wait():
        for half in range(2):
            rc(dbuf.at[0], dbuf.at[0], rg_s.at[0], rg_r.at[half], relays[half]).wait_recv()

    @pl.when(end)
    def _():
        for h in range(HEADS):
            for half in range(2):
                end_grad(h, half).start()

    for n in range(2):

        @pl.when(has[n])
        def _():
            do_copy(n, True, 1).start()

        @pl.when(plain[n])
        def _():
            do_copy(n, True, 0).start()

    grad_w(last)
    d_send(3)
    y_take(2)
    def backward(h):
        lanes = slice(h * HD, (h + 1) * HD)
        grads = d_out[lanes, :]
        delta = dl_out[h : h + 1, :]
        g = dot(vc[h], grads, 1, 0)
        ds = (probs[h].astype(F32) * (g - delta)).astype(BF16)
        ds_keep[h] = ds[0:TILE, :]
        gq = factor * dot(kc[h], ds, 0, 0)
        q_acc[:, lanes] = gq.T.astype(BF16)
        trows = slice(R_TXT, R_TXT + TXT)
        tx[0:TXT, lanes] = (factor * dot(ds[trows, :], qc[h, 0:TILE, :], 1, 0)).astype(BF16)
        tx[TXT : 2 * TXT, lanes] = dot(probs[h, trows, :], grads, 1, 1).astype(BF16)


    backward(0)
    y_send(3)
    backward(1)
    g_early(1)
    backward(2)
    q_out = pltpu.make_async_copy(q_acc, o_q, loc.at[6])
    q_out.start()
    t_go(0)
    relay_grads()
    g_early(2)
    y_take(3)
    t_go(1)
    g_early(3)
    for n in range(2):

        @pl.when(has[n])
        def _():
            do_copy(n, False, 1).wait_recv()

        @pl.when(plain[n])
        def _():
            do_copy(n, False, 0).wait_recv()

    @pl.when(end)
    def _():
        end_grad_wait()

    def own_keys(h):
        lanes = slice(h * HD, (h + 1) * HD)
        hrows = lanes
        gk = dot(ds_keep[h], qc[h, 0:TILE, :], 1, 0)
        gv = dot(probs[h, 0:TILE, :], d_out[hrows, :], 1, 1)
        for n in range(2):
            grads = d_near[n, hrows, :]
            p = pnear[n, h]
            g = dot(vc[h, 0:TILE, :], grads, 1, 0)
            ds = (p.astype(F32) * (g - dl_in[n, h : h + 1, :])).astype(BF16)
            gk += dot(ds, qc[h, TILE * (n + 1) : TILE * (n + 2), :], 1, 0)
            gv += dot(p, grads, 1, 1)
        k_acc[:, lanes] = (factor * gk).astype(BF16)
        v_acc[:, lanes] = gv.astype(BF16)

    g_late(1)
    own_keys(0)
    t_go(2)
    g_late(2)
    own_keys(1)
    g_early(4)
    t_go(3)
    own_keys(2)
    k_out = pltpu.make_async_copy(k_acc, o_k, loc.at[7])
    k_out.start()
    v_out = pltpu.make_async_copy(v_acc, o_v, loc.at[8])
    v_out.start()
    g_late(3)
    t_go(4)
    g_late(4)
    g_early(5)
    t_go(5)
    tk_out = pltpu.make_async_copy(t_fin.at[0:TXT], o_tk, loc.at[9])
    tk_out.start()
    tv_out = pltpu.make_async_copy(t_fin.at[TXT : 2 * TXT], o_tv, loc.at[10])
    tv_out.start()
    g_late(5)
    w_out = pltpu.make_async_copy(g_fin, o_w, loc.at[11])
    w_out.start()
    def drain_sends(ref, sem):
        rc(ref, ref, sem, zr.at[0, 0, 0], partner).wait_send()

    for d in range(2):
        drain_sends(sbuf.at[0:3], zs.at[d, 0])
        drain_sends(sbuf.at[0, 0:192], zs.at[d, 1])
    for c in (w_part, w_next, w_prev, *w_fwd, *y_sends):
        c.wait_send()
    for i in range(4):

        @pl.when(blocks[i] % 2 != core)
        def _():
            d_copy(i).wait_send()

    for c in (q_out, k_out, v_out, tk_out, tv_out, w_out):
        c.wait()
    for n in range(2):

        @pl.when(plain[n])
        def _():
            drain_sends(kc.at[:, 0 : 2 * TILE], hs_s.at[n])
            q_halo(n, True).wait_send()
            do_copy(n, True, 0).wait_send()

        @pl.when(has[n])
        def _():
            st_copy(n, True).wait_send()
            do_copy(n, True, 1).wait_send()

    @pl.when(end)
    def _():
        for half in range(2):
            drain_sends(rbuf.at[0], rs_s.at[half])
            drain_sends(dbuf.at[0], rd_s.at[half])

    @pl.when(relay)
    def _():
        for f in range(2):
            drain_sends(rbuf.at[f], rf_s.at[f])
            drain_sends(dbuf.at[f], rg_s.at[f])


def finish(*refs):
    given, results, held, wide, sems = refs[:6], refs[6:12], refs[12:18], refs[18], refs[19]
    loads = [pltpu.make_async_copy(given[i], held[i], sems.at[0, i]) for i in range(6)]
    for i in (5, 0, 1, 2, 3, 4):
        loads[i].start()
    stores = []
    for i in (5, 0, 1, 2, 3, 4):
        loads[i].wait()
        if i == 5:
            wide[...] = held[i][...].astype(F32)
            stores.append(pltpu.make_async_copy(wide, results[i], sems.at[1, i]))
        else:
            stores.append(pltpu.make_async_copy(held[i], results[i].at[0], sems.at[1, i]))
        stores[-1].start()
    for copy in stores:
        copy.wait()


def per_device(
    query, key, value, text_key, text_value, grad_out, gate, out_weight, windows, tile_map, text_count
):
    anyspec = pl.BlockSpec(memory_space=pl.ANY)
    vmem = pl.BlockSpec(memory_space=pltpu.VMEM)
    smem = pl.BlockSpec(memory_space=pltpu.SMEM)
    sds = jax.ShapeDtypeStruct
    v = pltpu.VMEM
    dma = pltpu.SemaphoreType.DMA
    out = pl.pallas_call(
        body,
        out_shape=(
            sds((TILE, TILE), BF16),
            sds((TILE, TILE), BF16),
            sds((TILE, TILE), BF16),
            sds((TXT, TILE), BF16),
            sds((TXT, TILE), BF16),
            sds((TILE, 768), BF16),
        ),
        in_specs=[anyspec] * 8 + [smem] * 3,
        out_specs=(anyspec,) * 6,
        scratch_shapes=[
            v((HEADS, QS, HD), BF16),
            v((HEADS, KEYS, HD), BF16),
            v((HEADS, KEYS, HD), BF16),
            v((TILE, TILE), BF16),
            v((N_TP, TILE, TILE), BF16),
            v((4, TILE, 768), BF16),
            v((HEADS, KEYS, TILE), F32),
            v((HEADS, KEYS, TILE), BF16),
            v((2, HEADS, TILE, TILE), BF16),
            v((HEADS, HD, TILE), BF16),
            v((TILE, TILE), BF16),
            v((TILE, TILE), F32),
            v((2, TILE, TILE), BF16),
            v((2, 8, TILE), F32),
            v((2, 8, TILE), F32),
            v((8, TILE), F32),
            v((2, 8, TILE), F32),
            v((8, TILE), F32),
            v((HEADS, TILE, TILE), BF16),
            v((4, TILE, 768), BF16),
            v((2, TILE, 768), BF16),
            v((TILE, 768), BF16),
            v((TILE, 768), BF16),
            v((TILE, 768), BF16),
            v((192, 768), BF16),
            v((96, 768), BF16),
            v((96, 768), BF16),
            v((96, 768), BF16),
            v((TILE, 768), BF16),
            v((2 * TXT, TILE), BF16),
            v((TXT, TILE), BF16),
            v((TXT // 2, TILE), BF16),
            v((TXT // 2, TILE), BF16),
            v((TXT // 2, TILE), BF16),
            v((2 * TXT, TILE), BF16),
            v((1, TILE), BF16),
            v((TILE, TILE), BF16),
            v((TILE, TILE), BF16),
            v((TILE, TILE), BF16),
            v((2, 9, 192, HD), BF16),
            v((2, HEADS, HD // 2, TILE), BF16),
            dma((12,)),
            dma((2, 2)),
            dma((2, 4, 2)),
            dma((2,)),
            dma((2, HEADS)),
            dma((2,)),
            dma((2,)),
            dma((2,)),
            dma((2,)),
            dma((2, 2)),
            dma((2, 2)),
            dma((5,)),
            dma((5,)),
            dma((4,)),
            dma((4,)),
            dma((2,)),
            dma((2,)),
            dma((9,)),
            dma((9,)),
            dma((9,)),
            dma((9,)),
            dma((2,)),
            dma((2, 4)),
            dma((2,)),
            dma((2, 4)),
            dma((2,)),
            dma((2, HEADS)),
            dma((2,)),
            dma((2,)),
        ],
        compiler_params=pltpu.CompilerParams(
            collective_id=0, has_side_effects=True, vmem_limit_bytes=60 * 1024 * 1024
        ),
    )(
        query[0], key[0], value[0], text_key[0], text_value[0], grad_out[0], gate, out_weight,
        windows.reshape(2), tile_map.reshape(8), text_count,
    )
    return pl.pallas_call(
        finish,
        out_shape=(
            sds((1, TILE, TILE), BF16),
            sds((1, TILE, TILE), BF16),
            sds((1, TILE, TILE), BF16),
            sds((1, TXT, TILE), BF16),
            sds((1, TXT, TILE), BF16),
            sds((TILE, 768), F32),
        ),
        in_specs=[anyspec] * 6,
        out_specs=(anyspec,) * 6,
        scratch_shapes=[
            v((TILE, TILE), BF16),
            v((TILE, TILE), BF16),
            v((TILE, TILE), BF16),
            v((TXT, TILE), BF16),
            v((TXT, TILE), BF16),
            v((TILE, 768), BF16),
            v((TILE, 768), F32),
            dma((2, 6)),
        ],
    )(*out)


def solution(mesh):
    placed = (
        P("dp", "sp", "tp"),
        P("dp", "sp", "tp"),
        P("dp", "sp", "tp"),
        P("dp", None, "tp"),
        P("dp", None, "tp"),
        P("dp", "sp", "tp"),
        P("dp", None),
        P("tp", "dp"),
        P("sp", None),
        P(),
        P("dp"),
    )
    return jax.shard_map(
        per_device,
        mesh=mesh,
        in_specs=placed,
        out_specs=(
            P("dp", "sp", "tp"),
            P("dp", "sp", "tp"),
            P("dp", "sp", "tp"),
            P("dp", None, "tp"),
            P("dp", None, "tp"),
            P("tp", "dp"),
        ),
        check_vma=False,
    )
```

time: 95.4 us -> 81.7 us (0.86)
  Pallas kernels: 92.6 us -> 79.2 us
  local copies, waits for them, and re-layouts: 1.32 us -> 0 us
    pallas_call x1, Pallas kernels: 89.6 us -> 76.5 us  [per_device(): pl.pallas_call(body, out_shape=(sds((TILE, TILE), BF16), sds((TILE, TILE)...]
    unnamed x1 -> x0, local copies, waits for them, and re-layouts: 1.32 us -> none
where the time goes in v3:
time: 81.7 us; the launch traced here: 80.6 us
  Pallas kernels  79.2 us (97%)
  between operations  1.45 us (2%)
    pallas_call x1, Pallas kernels, per_device(): pl.pallas_call(body, out_shape=(sds((TILE, TILE), BF16), sds((TILE, TILE)...  76.5 us
    pallas_call x1, Pallas kernels, per_device(): pl.pallas_call(finish, out_shape=(sds((1, TILE, TILE), BF16), sds((1, TIL...  2.67 us

profile of v3, /device:TPU:8, one launch (start us, length us, event | category | flops | bytes accessed | tf_op | source)
XLA Modules:
  0.0 80.6 jit_solution(2422543969214031233)
XLA Ops:
  1.3 76.5 %shard_map.154 = (bf16[384,384]{1,0:T(8,128)(2,1)}, bf16[384,384]{1,0:T(8,128)(2,1)}, bf16[384,384]{1,0:T(8,128)(2,1)}, bf16[256,384]{1,0:T(8,128)(2,1)}, bf16[2...) custom-call(bf16[384,384]{1,0:T(8,128)(2,1)} %bitcast.8, bf16[384,384]{1,0:T(8,128)(2,1)} %bitcast.9, ...), custom_call_target="tpu_custom_call" | custom-call | tf_op jit(solution)/shard_map/pallas_call | solution.py:719
  77.8 2.7 %shard_map.155 = (bf16[1,384,384]{2,1,0:T(8,128)(2,1)}, bf16[1,384,384]{2,1,0:T(8,128)(2,1)}, bf16[1,384,384]{2,1,0:T(8,128)(2,1)}, bf16[1,256,384]{2,1,0:T(8,12...) custom-call(bf16[384,384]{1,0:T(8,128)(2,1)} %get-tuple-element.12.refs_0_, ...), custom_call_target="tpu_custom_call" | custom-call | tf_op jit(solution)/shard_map/pallas_call | solution.py:810

commit v4 on v3

--- a/solution.py
+++ b/solution.py
@@ -33,7 +33,7 @@
     st_out, st_in, dl_out, dl_in, dl_own, ds_keep,
     gbuf, g_d, g_a, g_y, g_r, g_r1, g_r2, g_hs, g_rh, g_fin,
     tx, t_r1, t_r2, t_hs, t_rh, t_fin,
-    gate_ref, q_acc, k_acc, v_acc, rbuf, dbuf, loc, zs, zr, hs_s, hs_r, qs_s, qs_r, ss_s, ss_r, do_s, do_r, ws, wr,
+    gate_ref, q_acc, k_acc, v_acc, rbuf, dbuf, loc, zs, zr, hs_s, hs_r, qs_s, qs_r, ss_s, ss_r, do_s, do_r, dl_s, ws, wr,
     ds_, dr_, ys, yr, gs, gr, ts, tr, rs_s, rs_r, rf_s, rf_r, rd_s, rd_r, rg_s, rg_r,
 ):
     factor = HD ** (-0.5)
@@ -290,11 +290,21 @@
     z_service(1, (1,))
     forward(0)
     relay_pieces((2, 3))
-    w_next.start()
-    w_prev.start()
     w_part.start()
+
+    @pl.when(jnp.logical_not(relay))
+    def _():
+        w_next.start()
+        w_prev.start()
+
     forward(1)
     relay_pieces((4, 5))
+
+    @pl.when(relay)
+    def _():
+        w_next.start()
+        w_prev.start()
+
     z_service(2)
     forward(2)
     def st_copy(n, mine):
@@ -321,7 +331,7 @@
     g1 = (x % 2 + x // 2) % 2
     g2 = x // 2
 
-    def summer(src, fin, r1, r2, hs, rh, s_sem, r_sem):
+    def summer(src, fin, r1, r2, hs, rh, s_sem, r_sem, sent):
         rows = src.shape[0]
         part, half, quarter = rows // 2, rows // 4, rows // 8
 
@@ -337,20 +347,20 @@
         na2, nb2 = a1 + (1 - g2) * quarter, b1 + (1 - g1) * quarter
         copies = [
             (rc(at(src, na1, half), r1.at[0:half], s_sem.at[0], r_sem.at[0], p1),
-             rc(at(src, nb1, half), r1.at[half : 2 * half], s_sem.at[1], r_sem.at[1], p2)),
-            (rc(at(src, na2, quarter), r2.at[0:quarter], s_sem.at[2], r_sem.at[2], p2),
-             rc(at(src, nb2, quarter), r2.at[quarter : 2 * quarter], s_sem.at[3], r_sem.at[3], p1)),
-            (rc(hs, rh, s_sem.at[4], r_sem.at[4], across),),
-            (rc(at(fin, a2, quarter), at(fin, a2, quarter), s_sem.at[5], r_sem.at[5], p2),
-             rc(at(fin, b2, quarter), at(fin, b2, quarter), s_sem.at[6], r_sem.at[6], p1)),
-            (rc(at(fin, a1, half), at(fin, a1, half), s_sem.at[7], r_sem.at[7], p1),
-             rc(at(fin, b1, half), at(fin, b1, half), s_sem.at[8], r_sem.at[8], p2)),
+             rc(at(src, nb1, half), r1.at[half : 2 * half], s_sem.at[0], r_sem.at[1], p2)),
+            (rc(at(src, na2, quarter), r2.at[0:quarter], s_sem.at[0], r_sem.at[2], p2),
+             rc(at(src, nb2, quarter), r2.at[quarter : 2 * quarter], s_sem.at[0], r_sem.at[3], p1)),
+            (rc(hs, rh, s_sem.at[0], r_sem.at[4], across),),
+            (rc(at(fin, a2, quarter), at(fin, a2, quarter), s_sem.at[0], r_sem.at[5], p2),
+             rc(at(fin, b2, quarter), at(fin, b2, quarter), s_sem.at[0], r_sem.at[6], p1)),
+            (rc(at(fin, a1, half), at(fin, a1, half), s_sem.at[0], r_sem.at[7], p1),
+             rc(at(fin, b1, half), at(fin, b1, half), s_sem.at[0], r_sem.at[8], p2)),
         ]
         arrive = [
-            (rc(at(fin, na2, quarter), at(fin, na2, quarter), s_sem.at[5], r_sem.at[5], p2),
-             rc(at(fin, nb2, quarter), at(fin, nb2, quarter), s_sem.at[6], r_sem.at[6], p1)),
-            (rc(at(fin, na1, half), at(fin, na1, half), s_sem.at[7], r_sem.at[7], p1),
-             rc(at(fin, nb1, half), at(fin, nb1, half), s_sem.at[8], r_sem.at[8], p2)),
+            (rc(at(fin, na2, quarter), at(fin, na2, quarter), s_sem.at[0], r_sem.at[5], p2),
+             rc(at(fin, nb2, quarter), at(fin, nb2, quarter), s_sem.at[0], r_sem.at[6], p1)),
+            (rc(at(fin, na1, half), at(fin, na1, half), s_sem.at[0], r_sem.at[7], p1),
+             rc(at(fin, nb1, half), at(fin, nb1, half), s_sem.at[0], r_sem.at[8], p2)),
         ]
 
         def go(stage):
@@ -382,14 +392,12 @@
                 for c in copies[stage]:
                     c.start()
             else:
-                for group in copies:
-                    for c in group:
-                        c.wait_send()
+                rc(sent, sent, s_sem.at[0], r_sem.at[0], p1).wait_send()
 
         return go
 
-    g_go = summer(g_r, g_fin, g_r1, g_r2, g_hs, g_rh, gs, gr)
-    t_go = summer(tx, t_fin, t_r1, t_r2, t_hs, t_rh, ts, tr)
+    g_go = summer(g_r, g_fin, g_r1, g_r2, g_hs, g_rh, gs, gr, gbuf.at[0:2, 0:336])
+    t_go = summer(tx, t_fin, t_r1, t_r2, t_hs, t_rh, ts, tr, sbuf.at[0:4, 0:224])
 
     turn = 2 * (tp % 2) - 1
     blocks = tuple((tp // 2 + d + 4) % 4 for d in (0, turn, -turn, 2))
@@ -435,12 +443,12 @@
             g_go(0)
 
     def g_early(stage):
-        @pl.when(blocks[3] != dp)
+        @pl.when((blocks[0] == dp) | (blocks[1] == dp))
         def _():
             g_go(stage)
 
     def g_late(stage):
-        @pl.when(blocks[3] == dp)
+        @pl.when((blocks[2] == dp) | (blocks[3] == dp))
         def _():
             g_go(stage)
 
@@ -449,6 +457,33 @@
     grad_w((tp + 6) % N_TP)
     grad_w((tp + 2) % N_TP)
     d_send(1)
+    def near_all():
+        for n in range(2):
+
+            @pl.when(plain[n])
+            def _():
+                q_halo(n, False).wait_recv()
+
+            @pl.when(side(n))
+            def _():
+                end_wait(3)
+
+            @pl.when(has[n])
+            def _():
+                st_copy(n, False).wait_recv()
+
+            def near_probs(h, carry):
+                s = factor * dot(kc[h, 0:TILE, :], qc[h, TILE * (n + 1) : TILE * (n + 2), :], 1, 1)
+                p = jnp.exp(s - st_in[n, pl.ds(h, 1), :]) * st_in[n, pl.ds(h + 4, 1), :]
+                pnear[n, h] = p.astype(BF16)
+                return carry
+
+            lax.fori_loop(0, HEADS, near_probs, 0)
+
+
+    y_send(0)
+    relay_pieces((6, 7, 8))
+    z_service(3)
     w_fwd = []
     for half in range(2):
         rows = slice(half * 192, half * 192 + 192)
@@ -457,58 +492,46 @@
         fwd = rc(ref, ref, ws.at[3 + half], wr.at[3 + half], partner)
         fwd.start()
         w_fwd.append(fwd)
-    y_send(0)
+    y_send(1)
+    acc[...] = jnp.zeros_like(acc)
+    last = (tp + 4) % N_TP
+
+    def take_group(first):
+        def one(i, carry):
+            @pl.when(first + i != last)
+            def _():
+                acc[...] += take(first + i)
+
+            return carry
+
+        lax.fori_loop(0, 4, one, 0)
+
     mate = ylo * 2 + 1 - core
+    rc(wbuf.at[mate], wbuf.at[mate], ws.at[0], wr.at[0], partner).wait_recv()
+    take_group(ylo * 4)
+    grad_w((tp + 5) % N_TP)
+    grad_w((tp + 3) % N_TP)
+    d_send(2)
+
+    @pl.when(jnp.logical_not(end))
+    def _():
+        near_all()
+
     mate_other = (1 - ylo) * 2 + 1 - core
-    rc(wbuf.at[mate], wbuf.at[mate], ws.at[0], wr.at[0], partner).wait_recv()
     for half in range(2):
         ref = wbuf.at[mate_other, half * 192 : half * 192 + 192]
         rc(ref, ref, ws.at[3 + half], wr.at[3 + half], partner).wait_recv()
 
-    acc[...] = take(tp)
-
-    def more(h, carry):
-        acc[...] += take((tp + h + 1) % N_TP) + take((tp + N_TP - h - 1) % N_TP)
-        return carry
-
-    lax.fori_loop(0, 2, more, 0)
-
-    relay_pieces((6, 7, 8))
-    z_service(3)
-    more(2, 0)
-    grad_w((tp + 5) % N_TP)
-    grad_w((tp + 3) % N_TP)
-    d_send(2)
-    y_send(1)
-
-    for n in range(2):
-
-        @pl.when(plain[n])
-        def _():
-            q_halo(n, False).wait_recv()
-
-        @pl.when(side(n))
-        def _():
-            end_wait(3)
-
-        @pl.when(has[n])
-        def _():
-            st_copy(n, False).wait_recv()
-
-        def near_probs(h, carry):
-            s = factor * dot(kc[h, 0:TILE, :], qc[h, TILE * (n + 1) : TILE * (n + 2), :], 1, 1)
-            p = jnp.exp(s - st_in[n, pl.ds(h, 1), :]) * st_in[n, pl.ds(h + 4, 1), :]
-            pnear[n, h] = p.astype(BF16)
-            return carry
-
-        lax.fori_loop(0, HEADS, near_probs, 0)
-
+    take_group(4 - ylo * 4)
+    @pl.when(end)
+    def _():
+        near_all()
+
+    y_take(0)
     y_send(2)
-    y_take(0)
     y_take(1)
     z_wait(3, 0, 0)
     z_wait(3, 1, 1)
-    last = (tp + 4) % N_TP
     total = acc[...] + take(last)
     d_out[...] = total.astype(BF16)
     dl_out[...] = jnp.zeros((8, TILE), F32)
@@ -516,10 +539,14 @@
         both = d_out[h * HD : (h + 1) * HD, :].astype(F32) * att[h].astype(F32)
         dl_out[h : h + 1, :] = jnp.sum(both, axis=0, keepdims=True)
 
-    def do_copy(n, mine, which):
+    def do_copy(n, mine, h):
         to = 1 - n if mine else n
-        src, dst = ((d_out, d_near.at[to]), (dl_out, dl_in.at[to]))[which]
-        return rc(src, dst, do_s.at[n, which], do_r.at[to, which], near_dev[n])
+        rows = slice(h * HD, h * HD + HD)
+        return rc(d_out.at[rows], d_near.at[to, rows], do_s.at[n], do_r.at[to, h], near_dev[n])
+
+    def dl_copy(n, mine):
+        to = 1 - n if mine else n
+        return rc(dl_out, dl_in.at[to], dl_s.at[n], do_r.at[to, 3], near_dev[n])
 
     half_rows = HD // 2
 
@@ -532,41 +559,51 @@
     def forward_grad(h, f):
         rows = pl.ds(pl.multiple_of(h * HD + relay_half * half_rows, 16), half_rows)
         return rc(
-            dbuf.at[f, h], d_near.at[f, rows, :], rg_s.at[f], rg_r.at[relay_half], relay_to[f]
+            dbuf.at[f, h], d_near.at[f, rows, :], rg_s.at[f], rg_r.at[relay_half, h], relay_to[f]
         )
 
-    def relay_grads():
+    def relay_grads(h):
         @pl.when(relay)
         def _():
-            for h in range(HEADS):
-                for f in range(2):
-                    ref = dbuf.at[f, h]
-                    rc(ref, ref, rg_s.at[f], rd_r.at[f, h], relay_to[1 - f]).wait_recv()
-                    forward_grad(h, f).start()
-
-    def end_grad_wait():
-        for half in range(2):
-            rc(dbuf.at[0], dbuf.at[0], rg_s.at[0], rg_r.at[half], relays[half]).wait_recv()
-
-    @pl.when(end)
-    def _():
-        for h in range(HEADS):
+            for f in range(2):
+                ref = dbuf.at[f, h]
+                rc(ref, ref, rg_s.at[f], rd_r.at[f, h], relay_to[1 - f]).wait_recv()
+                forward_grad(h, f).start()
+
+    def send_grads(h):
+        @pl.when(end)
+        def _():
             for half in range(2):
                 end_grad(h, half).start()
 
+        for n in range(2):
+
+            @pl.when(plain[n])
+            def _():
+                do_copy(n, True, h).start()
+
+    def wait_grads(h):
+        @pl.when(end)
+        def _():
+            for half in range(2):
+                ref = dbuf.at[0, h]
+                rc(ref, ref, rg_s.at[0], rg_r.at[half, h], relays[half]).wait_recv()
+
+        for n in range(2):
+
+            @pl.when(plain[n])
+            def _():
+                do_copy(n, False, h).wait_recv()
+
     for n in range(2):
 
         @pl.when(has[n])
         def _():
-            do_copy(n, True, 1).start()
-
-        @pl.when(plain[n])
-        def _():
-            do_copy(n, True, 0).start()
-
+            dl_copy(n, True).start()
+
+    send_grads(0)
     grad_w(last)
     d_send(3)
-    y_take(2)
     def backward(h):
         lanes = slice(h * HD, (h + 1) * HD)
         grads = d_out[lanes, :]
@@ -582,31 +619,26 @@
 
 
     backward(0)
+    backward(1)
     y_send(3)
-    backward(1)
-    g_early(1)
     backward(2)
     q_out = pltpu.make_async_copy(q_acc, o_q, loc.at[6])
     q_out.start()
     t_go(0)
-    relay_grads()
+    g_early(1)
+    y_take(2)
+    send_grads(1)
     g_early(2)
     y_take(3)
+    send_grads(2)
+    relay_grads(0)
     t_go(1)
-    g_early(3)
+    relay_grads(1)
     for n in range(2):
 
         @pl.when(has[n])
         def _():
-            do_copy(n, False, 1).wait_recv()
-
-        @pl.when(plain[n])
-        def _():
-            do_copy(n, False, 0).wait_recv()
-
-    @pl.when(end)
-    def _():
-        end_grad_wait()
+            dl_copy(n, False).wait_recv()
 
     def own_keys(h):
         lanes = slice(h * HD, (h + 1) * HD)
@@ -623,13 +655,18 @@
         k_acc[:, lanes] = (factor * gk).astype(BF16)
         v_acc[:, lanes] = gv.astype(BF16)
 
+    wait_grads(0)
+    own_keys(0)
     g_late(1)
-    own_keys(0)
+    relay_grads(2)
+    g_early(3)
     t_go(2)
+    wait_grads(1)
+    own_keys(1)
     g_late(2)
-    own_keys(1)
     g_early(4)
     t_go(3)
+    wait_grads(2)
     own_keys(2)
     k_out = pltpu.make_async_copy(k_acc, o_k, loc.at[7])
     k_out.start()
@@ -637,8 +674,8 @@
     v_out.start()
     g_late(3)
     t_go(4)
+    g_early(5)
     g_late(4)
-    g_early(5)
     t_go(5)
     tk_out = pltpu.make_async_copy(t_fin.at[0:TXT], o_tk, loc.at[9])
     tk_out.start()
@@ -669,12 +706,12 @@
         def _():
             drain_sends(kc.at[:, 0 : 2 * TILE], hs_s.at[n])
             q_halo(n, True).wait_send()
-            do_copy(n, True, 0).wait_send()
+            drain_sends(d_out, do_s.at[n])
 
         @pl.when(has[n])
         def _():
             st_copy(n, True).wait_send()
-            do_copy(n, True, 1).wait_send()
+            dl_copy(n, True).wait_send()
 
     @pl.when(end)
     def _():
@@ -779,18 +816,19 @@
             dma((2,)),
             dma((2,)),
             dma((2,)),
-            dma((2, 2)),
-            dma((2, 2)),
+            dma((2,)),
+            dma((2, 4)),
+            dma((2,)),
             dma((5,)),
             dma((5,)),
             dma((4,)),
             dma((4,)),
             dma((2,)),
             dma((2,)),
+            dma((1,)),
             dma((9,)),
+            dma((1,)),
             dma((9,)),
-            dma((9,)),
-            dma((9,)),
             dma((2,)),
             dma((2, 4)),
             dma((2,)),
@@ -798,7 +836,7 @@
             dma((2,)),
             dma((2, HEADS)),
             dma((2,)),
-            dma((2,)),
+            dma((2, HEADS)),
         ],
         compiler_params=pltpu.CompilerParams(
             collective_id=0, has_side_effects=True, vmem_limit_bytes=60 * 1024 * 1024

time: 81.7 us -> 79.4 us (0.972)
  the two profiles are of different devices: /device:TPU:8 before, /device:TPU:56 now
where the time goes in v4:
time: 79.4 us; the launch traced here: 79.3 us
  Pallas kernels  77.8 us (98%)
  between operations  1.45 us (2%)
    pallas_call x1, Pallas kernels, per_device(): pl.pallas_call(body, out_shape=(sds((TILE, TILE), BF16), sds((TILE, TILE)...  75.1 us
    pallas_call x1, Pallas kernels, per_device(): pl.pallas_call(finish, out_shape=(sds((1, TILE, TILE), BF16), sds((1, TIL...  2.67 us

profile of v4, /device:TPU:56, one launch (start us, length us, event | category | flops | bytes accessed | tf_op | source)
XLA Modules:
  0.0 79.3 jit_solution(10384678463466663523)
XLA Ops:
  1.3 75.1 %shard_map.154 = (bf16[384,384]{1,0:T(8,128)(2,1)}, bf16[384,384]{1,0:T(8,128)(2,1)}, bf16[384,384]{1,0:T(8,128)(2,1)}, bf16[256,384]{1,0:T(8,128)(2,1)}, bf16[2...) custom-call(bf16[384,384]{1,0:T(8,128)(2,1)} %bitcast.8, bf16[384,384]{1,0:T(8,128)(2,1)} %bitcast.9, ...), custom_call_target="tpu_custom_call" | custom-call | tf_op jit(solution)/shard_map/pallas_call | solution.py:756
  76.4 2.7 %shard_map.155 = (bf16[1,384,384]{2,1,0:T(8,128)(2,1)}, bf16[1,384,384]{2,1,0:T(8,128)(2,1)}, bf16[1,384,384]{2,1,0:T(8,128)(2,1)}, bf16[1,256,384]{2,1,0:T(8,12...) custom-call(bf16[384,384]{1,0:T(8,128)(2,1)} %get-tuple-element.12.refs_0_, ...), custom_call_target="tpu_custom_call" | custom-call | tf_op jit(solution)/shard_map/pallas_call | solution.py:848

commit v5 on v4

--- a/solution.py
+++ b/solution.py
@@ -333,65 +333,72 @@
 
     def summer(src, fin, r1, r2, hs, rh, s_sem, r_sem, sent):
         rows = src.shape[0]
-        part, half, quarter = rows // 2, rows // 4, rows // 8
-
-        def at(ref, start, size):
-            return ref.at[pl.ds(pl.multiple_of(start, 16), size), :]
-
-        def rd(ref, start, size):
-            return ref[pl.ds(pl.multiple_of(start, 16), size), :].astype(F32)
-
-        a1, b1 = g1 * half, part + g2 * half
-        a2, b2 = a1 + g2 * quarter, b1 + g1 * quarter
-        na1, nb1 = (1 - g1) * half, part + (1 - g2) * half
-        na2, nb2 = a1 + (1 - g2) * quarter, b1 + (1 - g1) * quarter
-        copies = [
-            (rc(at(src, na1, half), r1.at[0:half], s_sem.at[0], r_sem.at[0], p1),
-             rc(at(src, nb1, half), r1.at[half : 2 * half], s_sem.at[0], r_sem.at[1], p2)),
-            (rc(at(src, na2, quarter), r2.at[0:quarter], s_sem.at[0], r_sem.at[2], p2),
-             rc(at(src, nb2, quarter), r2.at[quarter : 2 * quarter], s_sem.at[0], r_sem.at[3], p1)),
-            (rc(hs, rh, s_sem.at[0], r_sem.at[4], across),),
-            (rc(at(fin, a2, quarter), at(fin, a2, quarter), s_sem.at[0], r_sem.at[5], p2),
-             rc(at(fin, b2, quarter), at(fin, b2, quarter), s_sem.at[0], r_sem.at[6], p1)),
-            (rc(at(fin, a1, half), at(fin, a1, half), s_sem.at[0], r_sem.at[7], p1),
-             rc(at(fin, b1, half), at(fin, b1, half), s_sem.at[0], r_sem.at[8], p2)),
-        ]
-        arrive = [
-            (rc(at(fin, na2, quarter), at(fin, na2, quarter), s_sem.at[0], r_sem.at[5], p2),
-             rc(at(fin, nb2, quarter), at(fin, nb2, quarter), s_sem.at[0], r_sem.at[6], p1)),
-            (rc(at(fin, na1, half), at(fin, na1, half), s_sem.at[0], r_sem.at[7], p1),
-             rc(at(fin, nb1, half), at(fin, nb1, half), s_sem.at[0], r_sem.at[8], p2)),
-        ]
+        part, half, q = rows // 2, rows // 4, rows // 8
+
+        def at(ref, start):
+            return ref.at[pl.ds(pl.multiple_of(start, 16), q), :]
+
+        def rd(ref, start):
+            return ref[pl.ds(pl.multiple_of(start, 16), q), :].astype(F32)
+
+        def low(ref, i):
+            return ref[i * q : i * q + q, :].astype(F32)
+
+        def send(from_ref, start, to_ref, sem, dev):
+            return rc(at(from_ref, start), to_ref, s_sem.at[0], r_sem.at[sem], dev)
+
+        def same(start, sem, dev):
+            return send(fin, start, at(fin, start), sem, dev)
+
+        ka, kb = g1 * half + g2 * q, part + g2 * half + g1 * q
+        sa, sb = g1 * half + (1 - g2) * q, part + g2 * half + (1 - g1) * q
+        fa, fb = (1 - g1) * half + (1 - g2) * q, part + (1 - g2) * half + (1 - g1) * q
+        la, lb = (1 - g1) * half + g2 * q, part + (1 - g2) * half + g1 * q
+        first = (
+            send(src, fa, r1.at[0:q], 0, p1),
+            send(src, fb, r1.at[q : 2 * q], 1, p2),
+            send(src, la, r1.at[2 * q : 3 * q], 2, p1),
+            send(src, lb, r1.at[3 * q : 4 * q], 3, p2),
+        )
+        second = (
+            send(src, sa, r2.at[0:q], 4, p2),
+            send(src, sb, r2.at[q : 2 * q], 5, p1),
+        )
+        swap = rc(hs, rh, s_sem.at[0], r_sem.at[6], across)
+        spread = (same(ka, 7, p2), same(kb, 8, p1), same(ka, 9, p1), same(kb, 10, p2))
+        onward = (same(sa, 11, p1), same(sb, 12, p2))
+        near = (same(sa, 7, p2), same(sb, 8, p1))
+        far = (same(la, 9, p1), same(lb, 10, p2), same(fa, 11, p1), same(fb, 12, p2))
 
         def go(stage):
-            if stage == 1:
-                for c in copies[0]:
+            if stage == 0:
+                for c in first:
+                    c.start()
+            elif stage == 1:
+                for i, start in ((0, sa), (1, sb)):
+                    first[i].wait_recv()
+                    at(src, start)[...] = (rd(src, start) + low(r1, i)).astype(BF16)
+                    second[i].start()
+            elif stage == 2:
+                for i, start in ((0, ka), (1, kb)):
+                    first[2 + i].wait_recv()
+                    second[i].wait_recv()
+                    total = rd(src, start) + low(r1, 2 + i) + low(r2, i)
+                    hs[i * q : i * q + q, :] = total.astype(BF16)
+                swap.start()
+            elif stage == 3:
+                swap.wait_recv()
+                for i, start in ((0, ka), (1, kb)):
+                    at(fin, start)[...] = (low(hs, i) + low(rh, i)).astype(BF16)
+                for c in spread:
+                    c.start()
+            elif stage == 4:
+                for i in range(2):
+                    near[i].wait_recv()
+                    onward[i].start()
+            else:
+                for c in far:
                     c.wait_recv()
-                for start, low in ((a1, 0), (b1, half)):
-                    at(src, start, half)[...] = (
-                        rd(src, start, half) + r1[low : low + half, :].astype(F32)
-                    ).astype(BF16)
-            elif stage == 2:
-                for c in copies[1]:
-                    c.wait_recv()
-                for start, low in ((a2, 0), (b2, quarter)):
-                    hs[low : low + quarter, :] = (
-                        rd(src, start, quarter) + r2[low : low + quarter, :].astype(F32)
-                    ).astype(BF16)
-            elif stage == 3:
-                copies[2][0].wait_recv()
-                for start, low in ((a2, 0), (b2, quarter)):
-                    at(fin, start, quarter)[...] = (
-                        hs[low : low + quarter, :].astype(F32)
-                        + rh[low : low + quarter, :].astype(F32)
-                    ).astype(BF16)
-            elif stage >= 4:
-                for c in arrive[stage - 4]:
-                    c.wait_recv()
-            if stage < 5:
-                for c in copies[stage]:
-                    c.start()
-            else:
                 rc(sent, sent, s_sem.at[0], r_sem.at[0], p1).wait_send()
 
         return go
@@ -481,8 +488,27 @@
             lax.fori_loop(0, HEADS, near_probs, 0)
 
 
+    relay_pieces((6, 7, 8))
     y_send(0)
-    relay_pieces((6, 7, 8))
+    acc[...] = jnp.zeros_like(acc)
+    last = (tp + 4) % N_TP
+
+    def take_group(first, least, most):
+        def one(i, carry):
+            away = (first + i + N_TP - tp) % N_TP
+            away = jnp.minimum(away, N_TP - away)
+
+            @pl.when((away >= least) & (away <= most))
+            def _():
+                acc[...] += take(first + i)
+
+            return carry
+
+        lax.fori_loop(0, 4, one, 0)
+
+    mate = ylo * 2 + 1 - core
+    rc(wbuf.at[mate], wbuf.at[mate], ws.at[0], wr.at[0], partner).wait_recv()
+    take_group(ylo * 4, 0, 2)
     z_service(3)
     w_fwd = []
     for half in range(2):
@@ -493,22 +519,7 @@
         fwd.start()
         w_fwd.append(fwd)
     y_send(1)
-    acc[...] = jnp.zeros_like(acc)
-    last = (tp + 4) % N_TP
-
-    def take_group(first):
-        def one(i, carry):
-            @pl.when(first + i != last)
-            def _():
-                acc[...] += take(first + i)
-
-            return carry
-
-        lax.fori_loop(0, 4, one, 0)
-
-    mate = ylo * 2 + 1 - core
-    rc(wbuf.at[mate], wbuf.at[mate], ws.at[0], wr.at[0], partner).wait_recv()
-    take_group(ylo * 4)
+    take_group(ylo * 4, 3, 3)
     grad_w((tp + 5) % N_TP)
     grad_w((tp + 3) % N_TP)
     d_send(2)
@@ -522,7 +533,7 @@
         ref = wbuf.at[mate_other, half * 192 : half * 192 + 192]
         rc(ref, ref, ws.at[3 + half], wr.at[3 + half], partner).wait_recv()
 
-    take_group(4 - ylo * 4)
+    take_group(4 - ylo * 4, 0, 3)
     @pl.when(end)
     def _():
         near_all()
@@ -628,12 +639,13 @@
     g_early(1)
     y_take(2)
     send_grads(1)
+    relay_grads(0)
     g_early(2)
     y_take(3)
     send_grads(2)
-    relay_grads(0)
+    relay_grads(1)
     t_go(1)
-    relay_grads(1)
+    relay_grads(2)
     for n in range(2):
 
         @pl.when(has[n])
@@ -655,24 +667,23 @@
         k_acc[:, lanes] = (factor * gk).astype(BF16)
         v_acc[:, lanes] = gv.astype(BF16)
 
+    g_late(1)
+    g_early(3)
+    t_go(2)
     wait_grads(0)
     own_keys(0)
-    g_late(1)
-    relay_grads(2)
-    g_early(3)
-    t_go(2)
-    wait_grads(1)
-    own_keys(1)
     g_late(2)
     g_early(4)
     t_go(3)
+    wait_grads(1)
+    own_keys(1)
+    g_late(3)
     wait_grads(2)
     own_keys(2)
     k_out = pltpu.make_async_copy(k_acc, o_k, loc.at[7])
     k_out.start()
     v_out = pltpu.make_async_copy(v_acc, o_v, loc.at[8])
     v_out.start()
-    g_late(3)
     t_go(4)
     g_early(5)
     g_late(4)
@@ -826,9 +837,9 @@
             dma((2,)),
             dma((2,)),
             dma((1,)),
-            dma((9,)),
+            dma((13,)),
             dma((1,)),
-            dma((9,)),
+            dma((13,)),
             dma((2,)),
             dma((2, 4)),
             dma((2,)),

time: 79.4 us -> 77.4 us (0.975)
  the two profiles are of different devices: /device:TPU:56 before, /device:TPU:40 now
where the time goes in v5:
time: 77.4 us; the launch traced here: 77.2 us
  Pallas kernels  75.7 us (98%)
  between operations  1.45 us (2%)
    pallas_call x1, Pallas kernels, per_device(): pl.pallas_call(body, out_shape=(sds((TILE, TILE), BF16), sds((TILE, TILE)...  73.1 us
    pallas_call x1, Pallas kernels, per_device(): pl.pallas_call(finish, out_shape=(sds((1, TILE, TILE), BF16), sds((1, TIL...  2.67 us

profile of v5, /device:TPU:40, one launch (start us, length us, event | category | flops | bytes accessed | tf_op | source)
XLA Modules:
  0.0 77.2 jit_solution(9038622495419145871)
XLA Ops:
  1.3 73.1 %shard_map.154 = (bf16[384,384]{1,0:T(8,128)(2,1)}, bf16[384,384]{1,0:T(8,128)(2,1)}, bf16[384,384]{1,0:T(8,128)(2,1)}, bf16[256,384]{1,0:T(8,128)(2,1)}, bf16[2...) custom-call(bf16[384,384]{1,0:T(8,128)(2,1)} %bitcast.8, bf16[384,384]{1,0:T(8,128)(2,1)} %bitcast.9, ...), custom_call_target="tpu_custom_call" | custom-call | tf_op jit(solution)/shard_map/pallas_call | solution.py:767
  74.4 2.7 %shard_map.155 = (bf16[1,384,384]{2,1,0:T(8,128)(2,1)}, bf16[1,384,384]{2,1,0:T(8,128)(2,1)}, bf16[1,384,384]{2,1,0:T(8,128)(2,1)}, bf16[1,256,384]{2,1,0:T(8,12...) custom-call(bf16[384,384]{1,0:T(8,128)(2,1)} %get-tuple-element.12.refs_0_, ...), custom_call_target="tpu_custom_call" | custom-call | tf_op jit(solution)/shard_map/pallas_call | solution.py:859

commit v6 on v5

--- a/solution.py
+++ b/solution.py
@@ -150,14 +150,14 @@
 
     for u in range(2):
         for d in range(2):
-            z_unit(0, u, d).start()
+            z_unit(0, u ^ d, d).start()
 
     def z_service(k, units=(0, 1)):
         for u in units:
             for d in range(2):
-                z_wait(k - 1, u, d)
-                if k < 3 or u == d:
-                    z_unit(k, u, d).start()
+                z_wait(k - 1, u ^ d, d)
+                if k < 3 or u == 0:
+                    z_unit(k, u ^ d, d).start()
 
     def drain(ref, sem):
         pltpu.make_async_copy(ref, ref, sem).wait()
@@ -183,8 +183,8 @@
     drain(qc.at[:, 0:TILE], loc.at[4])
     wcopy.wait()
     w_part = rc(wbuf.at[dp], wbuf.at[dp], ws.at[0], wr.at[0], partner)
-    w_next = rc(wbuf.at[dp, 0:192], wbuf.at[dp, 0:192], ws.at[1], wr.at[1], y_next)
-    w_prev = rc(wbuf.at[dp, 192:384], wbuf.at[dp, 192:384], ws.at[2], wr.at[2], y_prev)
+    w_next = rc(wbuf.at[dp, 0:192], wbuf.at[dp, 0:192], ws.at[0], wr.at[1], y_next)
+    w_prev = rc(wbuf.at[dp, 192:384], wbuf.at[dp, 192:384], ws.at[0], wr.at[2], y_prev)
     def side(n):
         return (sp == 4) if n == 0 else (sp == 3)
 
@@ -199,13 +199,13 @@
         rows = slice(half * 192, half * 192 + 192)
         return rc(
             piece_src(piece).at[rows], rbuf.at[flow, piece],
-            rs_s.at[half], rs_r.at[flow, min(piece // 2, 3)], relays[half],
+            rs_s.at[0], rs_r.at[flow, min(piece // 2, 3)], relays[half],
         )
 
     def forward_piece(piece, f):
         start = (R_NEAR[0] if piece < 6 else TILE) + f * TILE + relay_half * 192
         dst = piece_src(piece).at[pl.ds(pl.multiple_of(start, 16), 192), :]
-        return rc(rbuf.at[f, piece], dst, rf_s.at[f], rf_r.at[relay_half, min(piece // 2, 3)], relay_to[f])
+        return rc(rbuf.at[f, piece], dst, rf_s.at[0], rf_r.at[relay_half, min(piece // 2, 3)], relay_to[f])
 
     def relay_pieces(pieces):
         @pl.when(relay)
@@ -213,7 +213,7 @@
             group = min(pieces[0] // 2, 3)
             for f in range(2):
                 ref = rbuf.at[f, pieces[0] : pieces[-1] + 1]
-                rc(ref, ref, rf_s.at[f], rs_r.at[f, group], relay_to[1 - f]).wait_recv()
+                rc(ref, ref, rf_s.at[0], rs_r.at[f, group], relay_to[1 - f]).wait_recv()
                 for piece in pieces:
                     forward_piece(piece, f).start()
 
@@ -358,17 +358,17 @@
             send(src, fa, r1.at[0:q], 0, p1),
             send(src, fb, r1.at[q : 2 * q], 1, p2),
             send(src, la, r1.at[2 * q : 3 * q], 2, p1),
-            send(src, lb, r1.at[3 * q : 4 * q], 3, p2),
+            send(src, lb, r1.at[3 * q : 4 * q], 2, p2),
         )
         second = (
-            send(src, sa, r2.at[0:q], 4, p2),
-            send(src, sb, r2.at[q : 2 * q], 5, p1),
-        )
-        swap = rc(hs, rh, s_sem.at[0], r_sem.at[6], across)
-        spread = (same(ka, 7, p2), same(kb, 8, p1), same(ka, 9, p1), same(kb, 10, p2))
-        onward = (same(sa, 11, p1), same(sb, 12, p2))
-        near = (same(sa, 7, p2), same(sb, 8, p1))
-        far = (same(la, 9, p1), same(lb, 10, p2), same(fa, 11, p1), same(fb, 12, p2))
+            send(src, sa, r2.at[0:q], 2, p2),
+            send(src, sb, r2.at[q : 2 * q], 2, p1),
+        )
+        swap = rc(hs, rh, s_sem.at[0], r_sem.at[3], across)
+        spread = (same(ka, 4, p2), same(kb, 5, p1), same(ka, 6, p1), same(kb, 6, p2))
+        onward = (same(sa, 6, p1), same(sb, 6, p2))
+        near = (same(sa, 4, p2), same(sb, 5, p1))
+        far = rc(r1, r1, s_sem.at[0], r_sem.at[6], p1)
 
         def go(stage):
             if stage == 0:
@@ -380,9 +380,8 @@
                     at(src, start)[...] = (rd(src, start) + low(r1, i)).astype(BF16)
                     second[i].start()
             elif stage == 2:
+                rc(r1, r1, s_sem.at[0], r_sem.at[2], p1).wait_recv()
                 for i, start in ((0, ka), (1, kb)):
-                    first[2 + i].wait_recv()
-                    second[i].wait_recv()
                     total = rd(src, start) + low(r1, 2 + i) + low(r2, i)
                     hs[i * q : i * q + q, :] = total.astype(BF16)
                 swap.start()
@@ -397,8 +396,7 @@
                     near[i].wait_recv()
                     onward[i].start()
             else:
-                for c in far:
-                    c.wait_recv()
+                far.wait_recv()
                 rc(sent, sent, s_sem.at[0], r_sem.at[0], p1).wait_send()
 
         return go
@@ -411,7 +409,7 @@
 
     def d_copy(i):
         b = blocks[i]
-        return rc(gbuf.at[b], g_d.at[b // 2], ds_.at[i], dr_.at[i], partner)
+        return rc(gbuf.at[b], g_d.at[b // 2], ds_.at[0], dr_.at[i], partner)
 
     def d_send(i):
         @pl.when(blocks[i] % 2 != core)
@@ -420,7 +418,7 @@
 
     y_sends = [
         rc(g_a.at[0:192], g_y.at[0:192], ys.at[0], yr.at[0], y_next),
-        rc(g_a.at[192:384], g_y.at[192:384], ys.at[1], yr.at[1], y_prev),
+        rc(g_a.at[192:384], g_y.at[192:384], ys.at[0], yr.at[0], y_prev),
     ]
 
     def y_send(i):
@@ -444,8 +442,7 @@
     def y_take(i):
         @pl.when(blocks[i] == dp)
         def _():
-            for c in y_sends:
-                c.wait_recv()
+            rc(g_a, g_y, ys.at[0], yr.at[0], y_next).wait_recv()
             g_r[...] = (g_r[...].astype(F32) + g_y[...].astype(F32)).astype(BF16)
             g_go(0)
 
@@ -488,6 +485,7 @@
             lax.fori_loop(0, HEADS, near_probs, 0)
 
 
+    z_service(3, (0,))
     relay_pieces((6, 7, 8))
     y_send(0)
     acc[...] = jnp.zeros_like(acc)
@@ -509,29 +507,29 @@
     mate = ylo * 2 + 1 - core
     rc(wbuf.at[mate], wbuf.at[mate], ws.at[0], wr.at[0], partner).wait_recv()
     take_group(ylo * 4, 0, 2)
-    z_service(3)
     w_fwd = []
     for half in range(2):
         rows = slice(half * 192, half * 192 + 192)
         ref = wbuf.at[other, rows]
-        rc(ref, ref, ws.at[1 + half], wr.at[1 + half], y_next).wait_recv()
-        fwd = rc(ref, ref, ws.at[3 + half], wr.at[3 + half], partner)
+        rc(ref, ref, ws.at[0], wr.at[1 + half], y_next).wait_recv()
+        fwd = rc(ref, ref, ws.at[0], wr.at[3 + half], partner)
         fwd.start()
         w_fwd.append(fwd)
     y_send(1)
+    @pl.when(jnp.logical_not(end))
+    def _():
+        near_all()
+
+    z_service(3, (1,))
     take_group(ylo * 4, 3, 3)
     grad_w((tp + 5) % N_TP)
     grad_w((tp + 3) % N_TP)
     d_send(2)
 
-    @pl.when(jnp.logical_not(end))
-    def _():
-        near_all()
-
     mate_other = (1 - ylo) * 2 + 1 - core
     for half in range(2):
         ref = wbuf.at[mate_other, half * 192 : half * 192 + 192]
-        rc(ref, ref, ws.at[3 + half], wr.at[3 + half], partner).wait_recv()
+        rc(ref, ref, ws.at[0], wr.at[3 + half], partner).wait_recv()
 
     take_group(4 - ylo * 4, 0, 3)
     @pl.when(end)
@@ -564,13 +562,13 @@
     def end_grad(h, half):
         rows = slice(h * HD + half * half_rows, h * HD + (half + 1) * half_rows)
         return rc(
-            d_out.at[rows], dbuf.at[flow, h], rd_s.at[half], rd_r.at[flow, h], relays[half]
+            d_out.at[rows], dbuf.at[flow, h], rd_s.at[0], rd_r.at[flow, h], relays[half]
         )
 
     def forward_grad(h, f):
         rows = pl.ds(pl.multiple_of(h * HD + relay_half * half_rows, 16), half_rows)
         return rc(
-            dbuf.at[f, h], d_near.at[f, rows, :], rg_s.at[f], rg_r.at[relay_half, h], relay_to[f]
+            dbuf.at[f, h], d_near.at[f, rows, :], rg_s.at[0], rg_r.at[relay_half, h], relay_to[f]
         )
 
     def relay_grads(h):
@@ -578,15 +576,16 @@
         def _():
             for f in range(2):
                 ref = dbuf.at[f, h]
-                rc(ref, ref, rg_s.at[f], rd_r.at[f, h], relay_to[1 - f]).wait_recv()
+                rc(ref, ref, rg_s.at[0], rd_r.at[f, h], relay_to[1 - f]).wait_recv()
                 forward_grad(h, f).start()
 
-    def send_grads(h):
+    def relay_send(h):
         @pl.when(end)
         def _():
             for half in range(2):
                 end_grad(h, half).start()
 
+    def send_grads(h):
         for n in range(2):
 
             @pl.when(plain[n])
@@ -612,7 +611,7 @@
         def _():
             dl_copy(n, True).start()
 
-    send_grads(0)
+    relay_send(0)
     grad_w(last)
     d_send(3)
     def backward(h):
@@ -638,14 +637,14 @@
     t_go(0)
     g_early(1)
     y_take(2)
-    send_grads(1)
+    send_grads(0)
+    relay_send(1)
     relay_grads(0)
     g_early(2)
     y_take(3)
-    send_grads(2)
-    relay_grads(1)
+    relay_send(2)
     t_go(1)
-    relay_grads(2)
+    send_grads(1)
     for n in range(2):
 
         @pl.when(has[n])
@@ -668,7 +667,10 @@
         v_acc[:, lanes] = gv.astype(BF16)
 
     g_late(1)
+    relay_grads(1)
     g_early(3)
+    send_grads(2)
+    relay_grads(2)
     t_go(2)
     wait_grads(0)
     own_keys(0)
@@ -680,20 +682,20 @@
     g_late(3)
     wait_grads(2)
     own_keys(2)
-    k_out = pltpu.make_async_copy(k_acc, o_k, loc.at[7])
+    k_out = pltpu.make_async_copy(k_acc, o_k, loc.at[6])
     k_out.start()
-    v_out = pltpu.make_async_copy(v_acc, o_v, loc.at[8])
+    v_out = pltpu.make_async_copy(v_acc, o_v, loc.at[6])
     v_out.start()
     t_go(4)
     g_early(5)
     g_late(4)
     t_go(5)
-    tk_out = pltpu.make_async_copy(t_fin.at[0:TXT], o_tk, loc.at[9])
+    tk_out = pltpu.make_async_copy(t_fin.at[0:TXT], o_tk, loc.at[6])
     tk_out.start()
-    tv_out = pltpu.make_async_copy(t_fin.at[TXT : 2 * TXT], o_tv, loc.at[10])
+    tv_out = pltpu.make_async_copy(t_fin.at[TXT : 2 * TXT], o_tv, loc.at[6])
     tv_out.start()
     g_late(5)
-    w_out = pltpu.make_async_copy(g_fin, o_w, loc.at[11])
+    w_out = pltpu.make_async_copy(g_fin, o_w, loc.at[6])
     w_out.start()
     def drain_sends(ref, sem):
         rc(ref, ref, sem, zr.at[0, 0, 0], partner).wait_send()
@@ -701,16 +703,11 @@
     for d in range(2):
         drain_sends(sbuf.at[0:3], zs.at[d, 0])
         drain_sends(sbuf.at[0, 0:192], zs.at[d, 1])
-    for c in (w_part, w_next, w_prev, *w_fwd, *y_sends):
-        c.wait_send()
-    for i in range(4):
-
-        @pl.when(blocks[i] % 2 != core)
-        def _():
-            d_copy(i).wait_send()
-
-    for c in (q_out, k_out, v_out, tk_out, tv_out, w_out):
-        c.wait()
+    drain_sends(gbuf.at[0:3], ws.at[0])
+    drain_sends(g_a, ys.at[0])
+    drain_sends(gbuf.at[0:2], ds_.at[0])
+
+    drain(sbuf.at[:, 0:304], loc.at[6])
     for n in range(2):
 
         @pl.when(plain[n])
@@ -726,15 +723,13 @@
 
     @pl.when(end)
     def _():
-        for half in range(2):
-            drain_sends(rbuf.at[0], rs_s.at[half])
-            drain_sends(dbuf.at[0], rd_s.at[half])
+        drain_sends(rbuf, rs_s.at[0])
+        drain_sends(dbuf, rd_s.at[0])
 
     @pl.when(relay)
     def _():
-        for f in range(2):
-            drain_sends(rbuf.at[f], rf_s.at[f])
-            drain_sends(dbuf.at[f], rg_s.at[f])
+        drain_sends(rbuf, rf_s.at[0])
+        drain_sends(dbuf, rg_s.at[0])
 
 
 def finish(*refs):
@@ -818,7 +813,7 @@
             v((TILE, TILE), BF16),
             v((2, 9, 192, HD), BF16),
             v((2, HEADS, HD // 2, TILE), BF16),
-            dma((12,)),
+            dma((7,)),
             dma((2, 2)),
             dma((2, 4, 2)),
             dma((2,)),
@@ -830,23 +825,23 @@
             dma((2,)),
             dma((2, 4)),
             dma((2,)),
+            dma((1,)),
             dma((5,)),
-            dma((5,)),
+            dma((1,)),
             dma((4,)),
-            dma((4,)),
-            dma((2,)),
-            dma((2,)),
             dma((1,)),
-            dma((13,)),
             dma((1,)),
-            dma((13,)),
-            dma((2,)),
+            dma((1,)),
+            dma((7,)),
+            dma((1,)),
+            dma((7,)),
+            dma((1,)),
             dma((2, 4)),
-            dma((2,)),
+            dma((1,)),
             dma((2, 4)),
-            dma((2,)),
+            dma((1,)),
             dma((2, HEADS)),
-            dma((2,)),
+            dma((1,)),
             dma((2, HEADS)),
         ],
         compiler_params=pltpu.CompilerParams(

time: 77.4 us -> 75 us (0.969)
  the two profiles are of different devices: /device:TPU:40 before, /device:TPU:8 now
where the time goes in v6:
time: 75 us; the launch traced here: 74.6 us
  Pallas kernels  73.2 us (98%)
  between operations  1.45 us (2%)
    pallas_call x1, Pallas kernels, per_device(): pl.pallas_call(body, out_shape=(sds((TILE, TILE), BF16), sds((TILE, TILE)...  70.5 us
    pallas_call x1, Pallas kernels, per_device(): pl.pallas_call(finish, out_shape=(sds((1, TILE, TILE), BF16), sds((1, TIL...  2.67 us

profile of v6, /device:TPU:8, one launch (start us, length us, event | category | flops | bytes accessed | tf_op | source)
XLA Modules:
  0.0 74.6 jit_solution(4780907823787556022)
XLA Ops:
  1.3 70.5 %shard_map.154 = (bf16[384,384]{1,0:T(8,128)(2,1)}, bf16[384,384]{1,0:T(8,128)(2,1)}, bf16[384,384]{1,0:T(8,128)(2,1)}, bf16[256,384]{1,0:T(8,128)(2,1)}, bf16[2...) custom-call(bf16[384,384]{1,0:T(8,128)(2,1)} %bitcast.8, bf16[384,384]{1,0:T(8,128)(2,1)} %bitcast.9, ...), custom_call_target="tpu_custom_call" | custom-call | tf_op jit(solution)/shard_map/pallas_call | solution.py:762
  71.8 2.7 %shard_map.155 = (bf16[1,384,384]{2,1,0:T(8,128)(2,1)}, bf16[1,384,384]{2,1,0:T(8,128)(2,1)}, bf16[1,384,384]{2,1,0:T(8,128)(2,1)}, bf16[1,256,384]{2,1,0:T(8,12...) custom-call(bf16[384,384]{1,0:T(8,128)(2,1)} %get-tuple-element.12.refs_0_, ...), custom_call_target="tpu_custom_call" | custom-call | tf_op jit(solution)/shard_map/pallas_call | solution.py:854

commit v7 on v6

--- a/solution.py
+++ b/solution.py
@@ -680,13 +680,13 @@
     wait_grads(1)
     own_keys(1)
     g_late(3)
+    t_go(4)
     wait_grads(2)
     own_keys(2)
     k_out = pltpu.make_async_copy(k_acc, o_k, loc.at[6])
     k_out.start()
     v_out = pltpu.make_async_copy(v_acc, o_v, loc.at[6])
     v_out.start()
-    t_go(4)
     g_early(5)
     g_late(4)
     t_go(5)

time: 75 us -> 75 us (level)
  no operation moved by 1% of the time
where the time goes in v7:
time: 75 us; the launch traced here: 74.6 us
  Pallas kernels  73.2 us (98%)
  between operations  1.45 us (2%)
    pallas_call x1, Pallas kernels, per_device(): pl.pallas_call(body, out_shape=(sds((TILE, TILE), BF16), sds((TILE, TILE)...  70.5 us
    pallas_call x1, Pallas kernels, per_device(): pl.pallas_call(finish, out_shape=(sds((1, TILE, TILE), BF16), sds((1, TIL...  2.67 us

profile of v7, /device:TPU:8, one launch (start us, length us, event | category | flops | bytes accessed | tf_op | source)
XLA Modules:
  0.0 74.6 jit_solution(1265018698512337026)
XLA Ops:
  1.3 70.5 %shard_map.154 = (bf16[384,384]{1,0:T(8,128)(2,1)}, bf16[384,384]{1,0:T(8,128)(2,1)}, bf16[384,384]{1,0:T(8,128)(2,1)}, bf16[256,384]{1,0:T(8,128)(2,1)}, bf16[2...) custom-call(bf16[384,384]{1,0:T(8,128)(2,1)} %bitcast.8, bf16[384,384]{1,0:T(8,128)(2,1)} %bitcast.9, ...), custom_call_target="tpu_custom_call" | custom-call | tf_op jit(solution)/shard_map/pallas_call | solution.py:762
  71.8 2.7 %shard_map.155 = (bf16[1,384,384]{2,1,0:T(8,128)(2,1)}, bf16[1,384,384]{2,1,0:T(8,128)(2,1)}, bf16[1,384,384]{2,1,0:T(8,128)(2,1)}, bf16[1,256,384]{2,1,0:T(8,12...) custom-call(bf16[384,384]{1,0:T(8,128)(2,1)} %get-tuple-element.12.refs_0_, ...), custom_call_target="tpu_custom_call" | custom-call | tf_op jit(solution)/shard_map/pallas_call | solution.py:854
